TPU v7x, 512 devices: a whole 4x8x8 slice. The times are simulated.
512 devices in a mesh: corpus: 256 (over y, z, x), dim: 2 (over core).
Axes of the slice: x: 4, y: 8, z: 8, core: 2. Of those that a mesh axis runs over, the one named last changes fastest.
Arguments:
- queries: bfloat16 [128, 768], P('dim'), as said below
- corpus: bfloat16 [131072, 768], P('corpus', 'dim'), as said below
- candidates: int32 [128, 1024], P('dim'), may hold values from 0 to 131071
Outputs:
- log_probs: float32 [128, 1024], P('dim', 'corpus')
Inputs may be any that keep to these rules, and one draw needn't show every extreme that they name: `queries`: query rows have real entries of moderate size; their norms differ from row to row. `corpus`: corpus rows have real entries of moderate size; their norms differ from row to row.
All inputs are finite; a program needn't handle non-finite values.
Results may differ from a plain program's by a relative error of at most 0.00095.
Values may be sent and summed in bfloat16 or wider, within the bound.
No kernel may reach another device: no remote copies, remote signals or barrier semaphores. Data moves between devices by JAX's collectives and lax.ppermute only.
A program may use at most 64 MiB of HBM per device.

v0:
```python
import jax
import jax.numpy as jnp
from jax import lax
from jax.sharding import Mesh
from jax.sharding import PartitionSpec as P

CORPUS = ("corpus_0", "corpus_1", "corpus_2")


def sent_to_all(value, axis):
    copies = jnp.broadcast_to(value, (lax.axis_size(axis), *value.shape))
    return lax.all_to_all(copies, axis, split_axis=0, concat_axis=0, tiled=True)


def joined_along(blocks, dim):
    blocks = jnp.moveaxis(blocks, 0, dim)
    lengths = blocks.shape
    return blocks.reshape(*lengths[:dim], lengths[dim] * lengths[dim + 1], *lengths[dim + 2 :])


def gather_directly(value, axis, dim):
    blocks = sent_to_all(value, axis)
    return joined_along(blocks, dim)


def collected_together(value, axis):
    leaves = jax.tree.leaves(value)
    sequence = sorted(range(len(leaves)), key=lambda k: -leaves[k].size)
    width = (1, *leaves[sequence[0]].shape)[-1]
    lines = [
        jnp.pad(leaves[k].reshape(-1), (0, -leaves[k].size % width)).reshape(-1, width)
        for k in sequence
    ]
    both, at, found = (lax.all_gather(jnp.concatenate(lines), axis), 0, {})
    for k, line in zip(sequence, lines):
        section = both[:, at : at + len(line)].reshape(len(both), -1)
        found[k] = section[:, : leaves[k].size].reshape(-1, *leaves[k].shape)
        at += len(line)
    numbers = iter(range(len(leaves)))
    return jax.tree.map(lambda _: found[next(numbers)], value)


def merged_by_axis(value, axes, combine):
    for axis in axes:
        pieces = collected_together(value, axis)
        value = jax.tree.map(lambda part: part[0], pieces)
        for k in range(1, lax.axis_size(axis)):
            value = combine(value, jax.tree.map(lambda part: part[k], pieces))
    return value


def cut_along(value, dim, count):
    before, after = (value.shape[:dim], value.shape[dim + 1 :])
    return jnp.moveaxis(value.reshape(*before, count, -1, *after), dim, 0)


def sum_at_owner(value, axis, dim):
    blocks = cut_along(value, dim, lax.axis_size(axis))
    arrived = lax.all_to_all(blocks, axis, split_axis=0, concat_axis=0, tiled=True)
    return arrived.sum(axis=0)


def summed_rows(value, axes, dim):
    far, near = axes
    blocks = cut_along(value, dim, lax.axis_size(far))
    nearer = sum_at_owner(blocks, near, dim + 1)
    arrived = lax.all_to_all(nearer, far, split_axis=0, concat_axis=0, tiled=True)
    return arrived.sum(axis=0)


def combine_pair(first, second):
    peak = jnp.maximum(first[0], second[0])
    mass = first[1] * jnp.exp(first[0] - peak) + second[1] * jnp.exp(second[0] - peak)
    return (peak, mass)


def local_pair(scores):
    peak = jnp.max(scores, axis=1)
    mass = jnp.sum(jnp.exp(scores - peak[:, None]), axis=1)
    return (peak, mass)


def pick_owned(scores, indices, offset):
    height = scores.shape[0]
    count = scores.shape[1]
    width = indices.shape[1]
    local = indices - offset
    inside = (local >= 0) & (local < count)
    upper = scores.astype(jnp.bfloat16)
    remain = scores - upper.astype(jnp.float32)
    middle = remain.astype(jnp.bfloat16)
    lower = (remain - middle.astype(jnp.float32)).astype(jnp.bfloat16)
    pieces = jnp.stack([upper, middle, lower], axis=1)
    group = 8

    def select_block(packed):
        block_pieces, block_local = packed
        positions = lax.broadcasted_iota(jnp.int32, (1, 1, count), 2)
        onehot = (block_local[:, :, None] == positions).astype(jnp.bfloat16)
        return jnp.einsum("qkr,qcr->qck", onehot, block_pieces, preferred_element_type=jnp.float32)

    selected = lax.map(
        select_block,
        (
            pieces.reshape(height // group, group, 3, count),
            local.reshape(height // group, group, width),
        ),
    )
    selected = selected.reshape(height, 3, width)
    values = selected[:, 2, :] + selected[:, 1, :] + selected[:, 0, :]
    return jnp.where(inside, values, jnp.float32(0.0))


def body(queries, corpus, candidates):
    rows = corpus.shape[0]
    scores = lax.dot_general(
        queries,
        gather_directly(corpus, "dim", 1),
        (((1,), (1,)), ((), ())),
        preferred_element_type=jnp.float32,
    )
    peak, mass = merged_by_axis(local_pair(scores), CORPUS, combine_pair)
    own_lse = peak + jnp.log(mass)
    offset = lax.axis_index(CORPUS) * rows
    picked = pick_owned(scores, candidates, offset)
    logits = summed_rows(picked, (("corpus_0", "corpus_1"), "corpus_2"), 1)
    return logits - own_lse[:, None]


def solution(mesh):
    torus = Mesh(
        mesh.devices.reshape(8, 8, 4, mesh.shape["dim"]),
        ("corpus_0", "corpus_1", "corpus_2", "dim"),
    )
    return jax.shard_map(
        body,
        mesh=torus,
        in_specs=(P("dim", None), P(CORPUS, "dim"), P("dim", None)),
        out_specs=P("dim", CORPUS),
        check_vma=False,
    )
```

profile of v0, /device:TPU:8, one launch (start us, length us, event | category | flops | bytes accessed | tf_op | source)
XLA Modules:
  0.0 116.1 jit_solution(17309862684395491505)
XLA Ops:
  0.0 1.2 %copy.25 = bf16[512,384]{0,1:T(8,128)(2,1)S(1)} copy(bf16[512,384]{1,0:T(8,128)(2,1)} %param.6) | data formatting | bytes 786432 | tf_op args[1]
  1.2 0.9 broadcast_in_dim.18
  2.1 3.5 %all-to-all-start = ((bf16[2,512,384]{1,2,0:T(8,128)(2,1)}), bf16[2,512,384]{1,2,0:T(8,128)(2,1)S(1)}, u32[]{:S(2)}, u32[]{:S(2)}) async-start(bf16[2,512,384]{1,2,0:T(8,128)(2,1)} %broadcast_in_dim.18), calls=%async_computation | async-start | bytes 1572864 | tf_op jit(solution)/shard_map/all_to_all | solution.py:12
  5.7 1.9 %all-to-all-done = bf16[2,512,384]{1,2,0:T(8,128)(2,1)S(1)} async-done(((bf16[2,512,384]{1,2,0:T(8,128)(2,1)}), bf16[2,512,384]{1,2,0:T(8,128)(2,1)S(1)}, u32[]{:S(2)}, u32[]{:S(2)}) %all-to-all-start) | async-done | bytes 786464 | tf_op jit(solution)/shard_map/all_to_all | solution.py:12
  7.6 0.3 fusion.81
  8.0 0.2 exponential_reduce_fusion
  8.1 0.1 copy.26
  8.3 0.1 copy.27
  8.4 0.1 copy.28
  8.5 0.0 copy-done.1
  8.6 0.5 pad_maximum_fusion
  9.0 29.6 %while.10 = (s32[]{:T(128)}, f32[8,8,3,1024]{3,1,0,2:T(8,128)S(1)}, bf16[8,8,3,512]{3,2,1,0:T(4,128)(2,1)S(1)}, s32[8,8,1024]{2,1,0:T(8,128)S(1)}, s32[]{:T(128)}) while((s32[]{:T(128)}, f32[8,8,3,1024]{3,1,0,2:T(8,128)S(1)}, bf16[8,8,3,512]{3,2,1,0:T(4,128)(2,1)S(1)}, s32[8,8,1024]{2,1,0:T(8,128)S(1)}, s32[]{:T(128)}) %tuple.25), condition=%wide.region_1.0_spmd, body=%wide.region_0.0_spmd.sunk | while | flops 29360128 | bytes 458825 | solution.py:102
  9.1 3.6 %fusion.87 = f32[1,8,3,1024]{3,2,1,0:T(4,128)S(1)} fusion(s32[8,1024]{1,0:T(8,128)S(1)} %dynamic-slice_bitcast_fusion.2, bf16[8,8,3,512]{3,2,1,0:T(4,128)(2,1)S(1)} %get-tuple-element.87, s32[]{:T(128)} %get-tuple-element.80), kind=kOutput, calls=%fused_computation.3.clone.1 | convolution fusion | flops 29360128 | bytes 163844 | tf_op jit(solution)/shard_map/while/body/eval_jaxpr/qkr,qcr->qck/dot_general | solution.py:100
  12.7 0.1 copy_dynamic-update-slice_fusion.2
  12.8 3.6 %fusion.87 = f32[1,8,3,1024]{3,2,1,0:T(4,128)S(1)} fusion(s32[8,1024]{1,0:T(8,128)S(1)} %dynamic-slice_bitcast_fusion.2, bf16[8,8,3,512]{3,2,1,0:T(4,128)(2,1)S(1)} %get-tuple-element.87, s32[]{:T(128)} %get-tuple-element.80), kind=kOutput, calls=%fused_computation.3.clone.1 | convolution fusion | flops 29360128 | bytes 163844 | tf_op jit(solution)/shard_map/while/body/eval_jaxpr/qkr,qcr->qck/dot_general | solution.py:100
  16.4 0.1 copy_dynamic-update-slice_fusion.2
  16.5 3.6 %fusion.87 = f32[1,8,3,1024]{3,2,1,0:T(4,128)S(1)} fusion(s32[8,1024]{1,0:T(8,128)S(1)} %dynamic-slice_bitcast_fusion.2, bf16[8,8,3,512]{3,2,1,0:T(4,128)(2,1)S(1)} %get-tuple-element.87, s32[]{:T(128)} %get-tuple-element.80), kind=kOutput, calls=%fused_computation.3.clone.1 | convolution fusion | flops 29360128 | bytes 163844 | tf_op jit(solution)/shard_map/while/body/eval_jaxpr/qkr,qcr->qck/dot_general | solution.py:100
  20.0 0.1 copy_dynamic-update-slice_fusion.2
  20.2 3.6 %fusion.87 = f32[1,8,3,1024]{3,2,1,0:T(4,128)S(1)} fusion(s32[8,1024]{1,0:T(8,128)S(1)} %dynamic-slice_bitcast_fusion.2, bf16[8,8,3,512]{3,2,1,0:T(4,128)(2,1)S(1)} %get-tuple-element.87, s32[]{:T(128)} %get-tuple-element.80), kind=kOutput, calls=%fused_computation.3.clone.1 | convolution fusion | flops 29360128 | bytes 163844 | tf_op jit(solution)/shard_map/while/body/eval_jaxpr/qkr,qcr->qck/dot_general | solution.py:100
  23.7 0.1 copy_dynamic-update-slice_fusion.2
  23.8 3.6 %fusion.87 = f32[1,8,3,1024]{3,2,1,0:T(4,128)S(1)} fusion(s32[8,1024]{1,0:T(8,128)S(1)} %dynamic-slice_bitcast_fusion.2, bf16[8,8,3,512]{3,2,1,0:T(4,128)(2,1)S(1)} %get-tuple-element.87, s32[]{:T(128)} %get-tuple-element.80), kind=kOutput, calls=%fused_computation.3.clone.1 | convolution fusion | flops 29360128 | bytes 163844 | tf_op jit(solution)/shard_map/while/body/eval_jaxpr/qkr,qcr->qck/dot_general | solution.py:100
  27.4 0.1 copy_dynamic-update-slice_fusion.2
  27.5 3.6 %fusion.87 = f32[1,8,3,1024]{3,2,1,0:T(4,128)S(1)} fusion(s32[8,1024]{1,0:T(8,128)S(1)} %dynamic-slice_bitcast_fusion.2, bf16[8,8,3,512]{3,2,1,0:T(4,128)(2,1)S(1)} %get-tuple-element.87, s32[]{:T(128)} %get-tuple-element.80), kind=kOutput, calls=%fused_computation.3.clone.1 | convolution fusion | flops 29360128 | bytes 163844 | tf_op jit(solution)/shard_map/while/body/eval_jaxpr/qkr,qcr->qck/dot_general | solution.py:100
  31.1 0.1 copy_dynamic-update-slice_fusion.2
  31.2 3.6 %fusion.87 = f32[1,8,3,1024]{3,2,1,0:T(4,128)S(1)} fusion(s32[8,1024]{1,0:T(8,128)S(1)} %dynamic-slice_bitcast_fusion.2, bf16[8,8,3,512]{3,2,1,0:T(4,128)(2,1)S(1)} %get-tuple-element.87, s32[]{:T(128)} %get-tuple-element.80), kind=kOutput, calls=%fused_computation.3.clone.1 | convolution fusion | flops 29360128 | bytes 163844 | tf_op jit(solution)/shard_map/while/body/eval_jaxpr/qkr,qcr->qck/dot_general | solution.py:100
  34.8 0.1 copy_dynamic-update-slice_fusion.2
  34.9 3.6 %fusion.87 = f32[1,8,3,1024]{3,2,1,0:T(4,128)S(1)} fusion(s32[8,1024]{1,0:T(8,128)S(1)} %dynamic-slice_bitcast_fusion.2, bf16[8,8,3,512]{3,2,1,0:T(4,128)(2,1)S(1)} %get-tuple-element.87, s32[]{:T(128)} %get-tuple-element.80), kind=kOutput, calls=%fused_computation.3.clone.1 | convolution fusion | flops 29360128 | bytes 163844 | tf_op jit(solution)/shard_map/while/body/eval_jaxpr/qkr,qcr->qck/dot_general | solution.py:100
  38.5 0.1 copy_dynamic-update-slice_fusion.2
  38.6 0.1 fusion.7
  38.7 0.2 copy.30
  38.9 0.2 copy.31
  39.1 1.0 reshape.932
  40.1 4.3 %all-to-all-start.1 = ((f32[4,1,16384]{2,1,0:T(1,128)}), f32[4,1,16384]{2,1,0:T(1,128)S(1)}, u32[]{:S(2)}, u32[]{:S(2)}) async-start(f32[4,1,16384]{2,1,0:T(1,128)} %reshape.932), calls=%async_computation.1 | async-start | bytes 524288 | tf_op jit(solution)/shard_map/all_to_all | solution.py:59
  44.4 18.2 %all-gather.3 = f32[8,2,64]{2,1,0:T(2,128)S(1)} all-gather(f32[1,2,64]{2,1,0:T(2,128)S(1)} %maximum_bitcast_fusion), channel_id=2, replica_groups=mesh['corpus_0'=8,'corpus_1'=8,'corpus_2'=4,'dim'=2] {'corpus_0'}, dimensions={0}, use_global_device_ids=true | all-gather | bytes 4608 | tf_op jit(solution)/shard_map/all_gather | solution.py:34
  62.7 19.5 %all-gather.4 = f32[8,2,64]{2,1,0:T(2,128)S(1)} all-gather(f32[1,2,64]{2,1,0:T(2,128)S(1)} %maximum_bitcast_fusion.1), channel_id=3, replica_groups=mesh['corpus_0'=8,'corpus_1'=8,'corpus_2'=4,'dim'=2] {'corpus_1'}, dimensions={0}, use_global_device_ids=true | all-gather | bytes 4608 | tf_op jit(solution)/shard_map/all_gather | solution.py:34
  82.2 10.2 %all-gather.5 = f32[4,2,64]{2,1,0:T(2,128)S(1)} all-gather(f32[1,2,64]{2,1,0:T(2,128)S(1)} %maximum_bitcast_fusion.2), channel_id=4, replica_groups=mesh['corpus_0'=8,'corpus_1'=8,'corpus_2'=4,'dim'=2] {'corpus_2'}, dimensions={0}, use_global_device_ids=true | all-gather | bytes 2560 | tf_op jit(solution)/shard_map/all_gather | solution.py:34
  92.4 0.0 all-to-all-done.1
  92.4 0.5 broadcast.1
  92.9 1.4 %reduce = f32[4,16384]{1,0:T(4,128)S(1)} reduce(f32[4,1,16384]{2,1,0:T(1,128)S(1)} %all-to-all-done.1, f32[]{:T(128)} %broadcast.1), dimensions={1}, to_apply=%all_to_all.10.reduce_sub_computation | reduce | bytes 524292 | tf_op jit(solution)/shard_map/all_to_all | solution.py:59
  94.3 0.3 reshape.933
  94.6 0.1 copy.40
  94.7 0.8 reshape.934
  95.5 7.6 %all-to-all-start.2 = ((f32[64,1,256]{2,1,0:T(1,128)}), f32[64,1,256]{2,1,0:T(1,128)S(1)}, u32[]{:S(2)}, u32[]{:S(2)}) async-start(f32[64,1,256]{2,1,0:T(1,128)} %reshape.934), calls=%async_computation.2 | async-start | bytes 131072 | tf_op jit(solution)/shard_map/all_to_all | solution.py:67
  103.1 11.4 %all-to-all-done.2 = f32[64,1,256]{2,1,0:T(1,128)S(1)} async-done(((f32[64,1,256]{2,1,0:T(1,128)}), f32[64,1,256]{2,1,0:T(1,128)S(1)}, u32[]{:S(2)}, u32[]{:S(2)}) %all-to-all-start.2) | async-done | bytes 65568 | tf_op jit(solution)/shard_map/all_to_all | solution.py:67
  114.5 0.8 reduce.1
  115.3 0.1 reshape.935
  115.4 0.1 bitcast_reduce_fusion.1
  115.5 0.6 broadcast_subtract_fusion
  (20 shorter events, 0.2 us)
Async XLA Ops:
  0.0 7.6 %copy-start = (bf16[64,768]{1,0:T(8,128)(2,1)S(1)}, bf16[64,768]{1,0:T(8,128)(2,1)}, u32[]{:S(2)}) copy-start(bf16[64,768]{1,0:T(8,128)(2,1)} %param.5) | copy-start | bytes 294916
  2.1 5.5 %all-to-all-start = ((bf16[2,512,384]{1,2,0:T(8,128)(2,1)}), bf16[2,512,384]{1,2,0:T(8,128)(2,1)S(1)}, u32[]{:S(2)}, u32[]{:S(2)}) async-start(bf16[2,512,384]{1,2,0:T(8,128)(2,1)} %broadcast_in_dim.18), calls=%async_computation | async-start | bytes 1572864 | tf_op jit(solution)/shard_map/all_to_all | solution.py:12
  7.6 1.0 copy-start.1
  40.1 52.3 %all-to-all-start.1 = ((f32[4,1,16384]{2,1,0:T(1,128)}), f32[4,1,16384]{2,1,0:T(1,128)S(1)}, u32[]{:S(2)}, u32[]{:S(2)}) async-start(f32[4,1,16384]{2,1,0:T(1,128)} %reshape.932), calls=%async_computation.1 | async-start | bytes 524288 | tf_op jit(solution)/shard_map/all_to_all | solution.py:59
  95.5 19.0 %all-to-all-start.2 = ((f32[64,1,256]{2,1,0:T(1,128)}), f32[64,1,256]{2,1,0:T(1,128)S(1)}, u32[]{:S(2)}, u32[]{:S(2)}) async-start(f32[64,1,256]{2,1,0:T(1,128)} %reshape.934), calls=%async_computation.2 | async-start | bytes 131072 | tf_op jit(solution)/shard_map/all_to_all | solution.py:67
where the time goes:
time: 116 us
  blocking collectives  47.9 us (41%)
  matrix products  29.1 us (25%)
  starting transfers between devices  15.5 us (13%)
  waiting for transfers between devices  13.3 us (11%)
  local copies, waits for them, and re-layouts  6.23 us (5%)
  other arithmetic  3.72 us (3%)
    all_gather x3, blocking collectives, collected_together(): both, at, found = (lax.all_gather(jnp.concatenate(lines), axis), 0, {})  47.9 us
    dot_general x8, matrix products, select_block(): jnp.einsum('qkr,qcr->qck', onehot, block_pieces, preferred_element_type=j...  28.7 us
    all_to_all x1, waiting for transfers between devices, summed_rows(): lax.all_to_all(nearer, far, split_axis=0, concat_axis=0, tiled=True)  11.4 us
    all_to_all x1, starting transfers between devices, summed_rows(): lax.all_to_all(nearer, far, split_axis=0, concat_axis=0, tiled=True)  7.64 us
    all_to_all x1, starting transfers between devices, sum_at_owner(): lax.all_to_all(blocks, axis, split_axis=0, concat_axis=0, tiled=True)  4.29 us
    all_to_all x1, starting transfers between devices, sent_to_all(): return lax.all_to_all(copies, axis, split_axis=0, concat_axis=0, tiled=True)  3.53 us
    unnamed x9, local copies, waits for them, and re-layouts  3.4 us
  transfers between devices with their start and end apart: 3, of which 2 were waited for; matrix products, arithmetic and copies ran while one was open for 0% of the time, Pallas kernels for 0%

commit v1 on v0

v1 whole, which is shorter than its diff:
```python
import jax
import jax.numpy as jnp
from jax import lax
from jax.experimental import pallas as pl
from jax.experimental.pallas import tpu as pltpu
from jax.sharding import Mesh
from jax.sharding import PartitionSpec as P

CORPUS = ("corpus_0", "corpus_1", "corpus_2")
LANES = 128
LINES = 3


def lane_gather(table, lanes):
    return jnp.take_along_axis(table, lanes, axis=1, mode="promise_in_bounds")


def halves(queries, dim):
    half = queries.shape[1] // 2
    first, second = queries[:, :half], queries[:, half:]
    return jnp.where(dim == 0, first, second), jnp.where(dim == 0, second, first)


def matmul_nt(left, right):
    return lax.dot_general(left, right, (((1,), (1,)), ((), ())), preferred_element_type=jnp.float32)


def prepare(place_ref, queries_ref, corpus_ref, candidates_ref, partial_ref, theirs_ref, local_ref):
    mine, theirs_ref[...] = halves(queries_ref[...], place_ref[0])
    partial_ref[...] = matmul_nt(mine, corpus_ref[...])
    height = candidates_ref.shape[0]
    lane = lax.broadcasted_iota(jnp.int32, (height, LANES), 1)
    quarter = lane // (LANES // 4)
    for slot in range(4):
        source = 4 * (lane % (LANES // 4)) + slot
        for part in range(2):
            value = jnp.zeros((height, LANES), jnp.int32)
            for w in range(4):
                block = candidates_ref[:, pl.ds((4 * part + w) * LANES, LANES)]
                value = jnp.where(quarter == w, lane_gather(block, source), value)
            local_ref[:, pl.ds((2 * slot + part) * LANES, LANES)] = value - place_ref[1]


def pack(theirs_ref, other_ref, partial_ref, local_ref, out_ref):
    scores = partial_ref[...] + matmul_nt(theirs_ref[...], other_ref[...])
    height, count = scores.shape
    peak = jnp.max(scores, axis=1, keepdims=True)
    mass = jnp.sum(jnp.exp(scores - peak), axis=1, keepdims=True)

    def pick(column):
        local = local_ref[:, pl.ds(column * LANES, LANES)]
        block, lane = local >> 7, local & (LANES - 1)
        value = jnp.zeros((height, LANES), jnp.float32)
        for w in range(count // LANES):
            value = jnp.where(block == w, lane_gather(scores[:, w * LANES : (w + 1) * LANES], lane), value)
        return value

    for pair in range(2):
        for part in range(2):
            both = jnp.concatenate([pick(4 * pair + part), pick(4 * pair + 2 + part)], axis=0)
            out_ref[pl.ds(LANES * LINES * part + pair, LANES, stride=LINES), :] = both.T
    spread = jnp.concatenate([jnp.broadcast_to(peak, (height, LANES)), jnp.broadcast_to(mass, (height, LANES))], axis=0).T
    for part in range(2):
        out_ref[pl.ds(LANES * LINES * part + 2, LANES, stride=LINES), :] = spread


def finish(all_ref, out_ref):
    sources = all_ref.shape[0] // LINES
    stats = all_ref[pl.ds(2, sources, stride=LINES), :]
    peak = jnp.max(stats, axis=0, keepdims=True)
    mass = jnp.sum(jnp.exp(stats - peak) * pltpu.roll(stats, LANES // 2, 1), axis=0, keepdims=True)
    lse = (peak + jnp.log(mass))[:, : LANES // 2]
    for pair in range(2):
        picked = jnp.sum(all_ref[pl.ds(pair, sources, stride=LINES), :], axis=0, keepdims=True)
        out_ref[2 * pair : 2 * pair + 1, :] = picked[:, : LANES // 2] - lse
        out_ref[2 * pair + 1 : 2 * pair + 2, :] = picked[:, LANES // 2 :] - lse


VMEM = pl.BlockSpec(memory_space=pltpu.VMEM)
SMEM = pl.BlockSpec(memory_space=pltpu.SMEM)


def on_chip(value):
    return pltpu.with_memory_space_constraint(value, pltpu.VMEM)


def body(queries, corpus, candidates):
    rows, width = corpus.shape
    height, picks = candidates.shape
    size = lax.axis_size(CORPUS)
    place = jnp.stack([lax.axis_index("dim"), lax.axis_index(CORPUS) * rows]).astype(jnp.int32)
    other = lax.ppermute(corpus, "dim", [(0, 1), (1, 0)])
    partial, theirs, local = pl.pallas_call(
        prepare,
        out_shape=(
            pltpu.VMEM((height, rows), jnp.float32),
            pltpu.VMEM((height, width), queries.dtype),
            pltpu.VMEM((height, picks), jnp.int32),
        ),
        in_specs=[SMEM, VMEM, VMEM, VMEM],
        out_specs=(VMEM, VMEM, VMEM),
        cost_estimate=pl.CostEstimate(flops=2 * height * rows * width, bytes_accessed=2 * rows * width, transcendentals=0),
        name="prepare",
    )(place, queries, corpus, candidates)
    sent = pl.pallas_call(
        pack,
        out_shape=pltpu.VMEM((size * LINES, LANES), jnp.float32),
        in_specs=[VMEM, VMEM, VMEM, VMEM],
        out_specs=VMEM,
        name="pack",
    )(on_chip(theirs), on_chip(other), on_chip(partial), on_chip(local))
    arrived = lax.all_to_all(sent.reshape(size, 1, LINES * LANES), CORPUS, split_axis=0, concat_axis=0, tiled=True)
    out = pl.pallas_call(
        finish,
        out_shape=jax.ShapeDtypeStruct((picks // size, height), jnp.float32),
        in_specs=[VMEM],
        out_specs=VMEM,
        name="finish",
    )(on_chip(arrived.reshape(size * LINES, LANES)))
    return out.T


def solution(mesh):
    torus = Mesh(
        mesh.devices.reshape(8, 8, 4, mesh.shape["dim"]),
        (*CORPUS, "dim"),
    )
    return jax.shard_map(
        body,
        mesh=torus,
        in_specs=(P("dim", None), P(CORPUS, "dim"), P("dim", None)),
        out_specs=P("dim", CORPUS),
        check_vma=False,
    )
```

time: 116 us -> 45.9 us (0.40)
  matrix products: 29.1 us -> 0 us
  starting transfers between devices: 15.5 us -> 1.91 us
  waiting for transfers between devices: 13.3 us -> 0.01 us
  blocking collectives: 47.9 us -> 39.6 us
  local copies, waits for them, and re-layouts: 6.23 us -> 0 us
  Pallas kernels: 0 us -> 3.52 us
  other arithmetic: 3.72 us -> 0.65 us
    all_gather x3 -> x0, blocking collectives: 47.9 us -> none  [collected_together(): both, at, found = (lax.all_gather(jnp.concatenate(lines), axis), 0, {})]
    all_to_all x0 -> x1, blocking collectives: none -> 39.6 us  [body(): lax.all_to_all(sent.reshape(size, 1, LINES * LANES), CORPUS, split_axis=0...]
    dot_general x9 -> x0, matrix products: 29.1 us -> none  [the longest x8 28.7 us: select_block(): jnp.einsum('qkr,qcr->qck', onehot, block_pieces, preferred_element_type=j...]
    all_to_all x3 -> x0, starting transfers between devices: 15.5 us -> none  [the longest x1 7.64 us: summed_rows(): lax.all_to_all(nearer, far, split_axis=0, concat_axis=0, tiled=True)]
    all_to_all x3 -> x0, waiting for transfers between devices: 13.3 us -> none  [the longest x1 11.4 us: summed_rows(): lax.all_to_all(nearer, far, split_axis=0, concat_axis=0, tiled=True)]
    pallas_call x0 -> x3, Pallas kernels: none -> 3.52 us  [the longest x1 1.49 us: body(): pl.pallas_call(prepare, out_shape=(pltpu.VMEM((height, rows), jnp.float32...]
    unnamed x9 -> x0, local copies, waits for them, and re-layouts: 3.4 us -> none
    all_to_all x2 -> x0, other arithmetic: 2.17 us -> none  [the longest x1 1.37 us: sum_at_owner(): lax.all_to_all(blocks, axis, split_axis=0, concat_axis=0, tiled=True)]
  transfers between devices with their start and end apart: 3 -> 1, of which waited for: 2 -> 0; matrix products, arithmetic and copies ran while one was open for 0% -> 1% of each run, Pallas kernels for 0% -> 3%
where the time goes in v1:
time: 45.9 us; the launch traced here: 45.7 us
  blocking collectives  39.6 us (86%)
  Pallas kernels  3.52 us (8%)
  starting transfers between devices  1.91 us (4%)
  other arithmetic  0.65 us (1%)
    all_to_all x1, blocking collectives, body(): lax.all_to_all(sent.reshape(size, 1, LINES * LANES), CORPUS, split_axis=0...  39.6 us
    ppermute x1, starting transfers between devices, body(): other = lax.ppermute(corpus, 'dim', [(0, 1), (1, 0)])  1.91 us
    pallas_call x1, Pallas kernels, body(): pl.pallas_call(prepare, out_shape=(pltpu.VMEM((height, rows), jnp.float32...  1.49 us
    pallas_call x1, Pallas kernels, body(): pl.pallas_call(pack, out_shape=pltpu.VMEM((size * LINES, LANES), jnp.floa...  1.19 us
  transfers between devices with their start and end apart: 1, of which 0 were waited for; matrix products, arithmetic and copies ran while one was open for 1% of the time, Pallas kernels for 3%

profile of v1, /device:TPU:8, one launch (start us, length us, event | category | flops | bytes accessed | tf_op | source)
XLA Modules:
  0.0 45.7 jit_solution(10778207406425317302)
XLA Ops:
  0.0 1.9 %collective-permute-start = (bf16[512,384]{1,0:T(8,128)(2,1)}, bf16[512,384]{1,0:T(8,128)(2,1)S(1)}, u32[]{:S(2)}, u32[]{:S(2)}) collective-permute-start(bf16[512,384]{1,0:T(8,128)(2,1)} %corpus_ref.1), channel_id=1, source_target_pairs={{0,1},{1,0},{2,3},{3,2},{4,5},{5,4},{6,7},{7,6},{8,9},{9,8},{10,11... | collective-permute-start | bytes 1179656 | tf_op jit(solution)/shard_map/ppermute | solution.py:92
  1.9 0.6 %pad_add_fusion.place_ref = s32[2]{0:T(128)} fusion(s32[1]{0:T(128)} %bitcast.1, s32[1]{0:T(128)} %bitcast), kind=kLoop, calls=%fused_computation | loop fusion | flops 2 | bytes 16 | tf_op jit(solution)/shard_map/stack | solution.py:91
  2.6 1.5 %prepare.1 = (f32[64,512]{1,0:T(8,128)S(1)}, bf16[64,384]{1,0:T(8,128)(2,1)S(1)}, s32[64,1024]{1,0:T(8,128)S(1)}) custom-call(s32[2]{0:T(128)} %pad_add_fusion.place_ref, bf16[64,768]{1,0:T(8,128)(2,1)} %queries_ref.1, bf16[512,384]{1,0:T(8,128)(2,1)} %corpus_ref.1, s32[64,1024]{1,0:T(8,128)} %candidates_ref.1), custom_call_target="tpu_custom_call" | custom-call | flops 25165824 | bytes 393216 | tf_op jit(solution)/shard_map/prepare/pallas_call | solution.py:93
  4.1 0.0 collective-permute-done.other_ref
  4.1 1.2 %pack.1 = f32[768,128]{1,0:T(8,128)S(1)} custom-call(bf16[64,384]{1,0:T(8,128)(2,1)S(1)} %get-tuple-element.8.theirs_ref, bf16[512,384]{1,0:T(8,128)(2,1)S(1)} %collective-permute-done.other_ref, f32[64,512]{1,0:T(8,128)S(1)} %get-tuple-element.9.partial_ref, s32[64,1024]{1,0:T(8,128)S(1)} %get-tuple-element.10.local_ref), custom_call_target="tpu_custom_call" | custom-call | tf_op jit(solution)/shard_map/pack/pallas_call | solution.py:105
  5.3 39.6 %all_to_all.5 = f32[256,1,384]{2,1,0:T(1,128)S(1)} all-to-all(f32[256,1,384]{2,1,0:T(1,128)S(1)} %bitcast.6), channel_id=1, replica_groups=mesh['corpus_0'=8,'corpus_1'=8,'corpus_2'=4,'dim'=2] {'corpus_0','corpus..., dimensions={0} | all-to-all | bytes 786432 | tf_op jit(solution)/shard_map/all_to_all | solution.py:112
  44.8 0.8 %finish.1 = f32[4,64]{1,0:T(4,128)} custom-call(f32[768,128]{1,0:T(8,128)S(1)} %bitcast.5), custom_call_target="tpu_custom_call" | custom-call | tf_op jit(solution)/shard_map/finish/pallas_call | solution.py:113
Async XLA Ops:
  0.0 4.1 %collective-permute-start = (bf16[512,384]{1,0:T(8,128)(2,1)}, bf16[512,384]{1,0:T(8,128)(2,1)S(1)}, u32[]{:S(2)}, u32[]{:S(2)}) collective-permute-start(bf16[512,384]{1,0:T(8,128)(2,1)} %corpus_ref.1), channel_id=1, source_target_pairs={{0,1},{1,0},{2,3},{3,2},{4,5},{5,4},{6,7},{7,6},{8,9},{9,8},{10,11... | collective-permute-start | bytes 1179656 | tf_op jit(solution)/shard_map/ppermute | solution.py:92

commit v2 on v1

v2 whole, which is shorter than its diff:
```python
import jax
import jax.numpy as jnp
from jax import lax
from jax.experimental import pallas as pl
from jax.experimental.pallas import tpu as pltpu
from jax.sharding import Mesh
from jax.sharding import PartitionSpec as P

CORPUS = ("corpus_0", "corpus_1", "corpus_2")
LANES = 128
HALF = LANES // 2
LINES = 4


def lane_gather(table, lanes):
    return jnp.take_along_axis(table, lanes, axis=1, mode="promise_in_bounds")


def halves(queries, dim):
    half = queries.shape[1] // 2
    first, second = queries[:, :half], queries[:, half:]
    return jnp.where(dim == 0, first, second), jnp.where(dim == 0, second, first)


def matmul_nt(left, right):
    return lax.dot_general(left, right, (((1,), (1,)), ((), ())), preferred_element_type=jnp.float32)


def spread(column):
    return jnp.broadcast_to(column, (column.shape[0], LANES))


def rounded(value):
    return value.astype(jnp.bfloat16).astype(jnp.float32)


def prepare(queries_ref, corpus_ref, candidates_ref, partial_ref, theirs_ref, local_ref, owner_ref):
    mine, theirs_ref[...] = halves(queries_ref[...], lax.axis_index("dim"))
    partial_ref[...] = matmul_nt(mine, corpus_ref[...])
    height = candidates_ref.shape[0]
    rows = corpus_ref.shape[0]
    position = lax.axis_index(CORPUS)
    lane = lax.broadcasted_iota(jnp.int32, (height, LANES), 1)
    group = LANES // 4
    quarter = lane // group
    for slot in range(4):
        source = 4 * (lane % group) + slot
        for part in range(2):
            value = jnp.zeros((height, LANES), jnp.int32)
            for w in range(4):
                block = candidates_ref[:, pl.ds((4 * part + w) * LANES, LANES)]
                value = jnp.where(quarter == w, lane_gather(block, source), value)
            local_ref[:, pl.ds((2 * slot + part) * LANES, LANES)] = value - position * rows
    own = candidates_ref[:, pl.ds(pl.multiple_of(position // group * LANES, LANES), LANES)]
    at = jnp.full((height, LANES), 4 * (position % group), jnp.int32)
    for pair in range(2):
        both = jnp.concatenate([lane_gather(own, at + 2 * pair), lane_gather(own, at + 2 * pair + 1)], axis=0)
        owner_ref[pair : pair + 1, :] = (both.astype(jnp.float32).T)[:1, :].astype(jnp.int32) // rows


def pack(theirs_ref, other_ref, partial_ref, local_ref, out_ref, lines_ref):
    scores = partial_ref[...] + matmul_nt(theirs_ref[...], other_ref[...])
    height, count = scores.shape
    peak = jnp.max(scores, axis=1, keepdims=True)
    lse = peak + jnp.log(jnp.sum(jnp.exp(scores - peak), axis=1, keepdims=True))
    center = rounded(jnp.sum(scores, axis=1, keepdims=True) * (1.0 / count))
    moved = scores - center

    def pick(column):
        local = local_ref[:, pl.ds(column * LANES, LANES)]
        block, lane = local >> 7, local & (LANES - 1)
        value = jnp.zeros((height, LANES), jnp.float32)
        for w in range(count // LANES):
            value = jnp.where(block == w, lane_gather(moved[:, w * LANES : (w + 1) * LANES], lane), value)
        return value

    def write(line, part, value):
        lines_ref[pl.ds(LANES * LINES * part + line, LANES, stride=LINES), :] = value

    for pair in range(2):
        for part in range(2):
            both = jnp.concatenate([pick(4 * pair + part), pick(4 * pair + 2 + part)], axis=0)
            write(pair, part, both.T)
    upper = rounded(lse)
    middle = rounded(lse - upper)
    lower = lse - upper - middle
    first = jnp.concatenate([spread(upper), spread(middle)], axis=0).T
    second = jnp.concatenate([spread(lower), spread(center)], axis=0).T
    for part in range(2):
        write(2, part, first)
        write(3, part, second)
    out_ref[...] = lines_ref[...].astype(jnp.bfloat16)


def finish(all_ref, owner_ref, out_ref, lines_ref):
    lines_ref[...] = all_ref[...].astype(jnp.float32)
    sources = all_ref.shape[0] // LINES
    first = lines_ref[pl.ds(2, sources, stride=LINES), :]
    second = lines_ref[pl.ds(3, sources, stride=LINES), :]
    local = first + pltpu.roll(first, HALF, 1) + second
    low = lax.broadcasted_iota(jnp.int32, (1, LANES), 1) < HALF
    peak = jnp.max(local, axis=0, keepdims=True)
    mass = jnp.sum(jnp.exp(local - peak), axis=0, keepdims=True)
    lse = (peak + jnp.log(mass))[:, :HALF]
    center = jnp.where(low, pltpu.roll(second, HALF, 1), second)
    source = lax.broadcasted_iota(jnp.int32, (sources, LANES), 0)
    for pair in range(2):
        moved = lines_ref[pl.ds(pair, sources, stride=LINES), :]
        back = jnp.where(source == owner_ref[pair : pair + 1, :], center, 0.0)
        picked = jnp.sum(moved + back, axis=0, keepdims=True)
        out_ref[2 * pair : 2 * pair + 1, :] = picked[:, :HALF] - lse
        out_ref[2 * pair + 1 : 2 * pair + 2, :] = picked[:, HALF:] - lse


VMEM = pl.BlockSpec(memory_space=pltpu.VMEM)


def on_chip(value):
    return pltpu.with_memory_space_constraint(value, pltpu.VMEM)


def body(queries, corpus, candidates):
    rows, width = corpus.shape
    height, picks = candidates.shape
    size = lax.axis_size(CORPUS)
    other = lax.ppermute(corpus, "dim", [(0, 1), (1, 0)])
    partial, theirs, local, owner = pl.pallas_call(
        prepare,
        out_shape=(
            pltpu.VMEM((height, rows), jnp.float32),
            pltpu.VMEM((height, width), queries.dtype),
            pltpu.VMEM((height, picks), jnp.int32),
            pltpu.VMEM((2, LANES), jnp.int32),
        ),
        in_specs=[VMEM, VMEM, VMEM],
        out_specs=(VMEM, VMEM, VMEM, VMEM),
        cost_estimate=pl.CostEstimate(flops=2 * height * rows * width, bytes_accessed=2 * rows * width, transcendentals=0),
        name="prepare",
    )(queries, corpus, candidates)
    sent = pl.pallas_call(
        pack,
        out_shape=pltpu.VMEM((size * LINES, LANES), jnp.bfloat16),
        in_specs=[VMEM, VMEM, VMEM, VMEM],
        out_specs=VMEM,
        scratch_shapes=[pltpu.VMEM((size * LINES, LANES), jnp.float32)],
        name="pack",
    )(on_chip(theirs), on_chip(other), on_chip(partial), on_chip(local))
    arrived = lax.all_to_all(sent.reshape(size, LINES, LANES), CORPUS, split_axis=0, concat_axis=0, tiled=True)
    out = pl.pallas_call(
        finish,
        out_shape=jax.ShapeDtypeStruct((picks // size, height), jnp.float32),
        in_specs=[VMEM, VMEM],
        out_specs=VMEM,
        scratch_shapes=[pltpu.VMEM((size * LINES, LANES), jnp.float32)],
        name="finish",
    )(on_chip(arrived.reshape(size * LINES, LANES)), on_chip(owner))
    return out.T


def solution(mesh):
    torus = Mesh(
        mesh.devices.reshape(8, 8, 4, mesh.shape["dim"]),
        (*CORPUS, "dim"),
    )
    return jax.shard_map(
        body,
        mesh=torus,
        in_specs=(P("dim", None), P(CORPUS, "dim"), P("dim", None)),
        out_specs=P("dim", CORPUS),
        check_vma=False,
    )
```

time: 45.9 us -> 43.5 us (0.948)
  blocking collectives: 39.6 us -> 37.3 us
  other arithmetic: 0.65 us -> 0 us
    all_to_all x1, blocking collectives: 39.6 us -> 37.3 us  [body(): lax.all_to_all(sent.reshape(size, LINES, LANES), CORPUS, split_axis=0, co...]
    another operation x1 -> x0, other arithmetic: 0.65 us -> none  [body(): jnp.stack([lax.axis_index('dim'), lax.axis_index(CORPUS) * rows])]
  transfers between devices with their start and end apart: 1 -> 1, of which waited for: 0 -> 1; matrix products, arithmetic and copies ran while one was open for 1% -> 0% of each run, Pallas kernels for 3% -> 4%
where the time goes in v2:
time: 43.5 us; the launch traced here: 43.3 us
  blocking collectives  37.3 us (86%)
  Pallas kernels  3.74 us (9%)
  starting transfers between devices  1.91 us (4%)
    all_to_all x1, blocking collectives, body(): lax.all_to_all(sent.reshape(size, LINES, LANES), CORPUS, split_axis=0, co...  37.3 us
    ppermute x1, starting transfers between devices, body(): other = lax.ppermute(corpus, 'dim', [(0, 1), (1, 0)])  1.91 us
    pallas_call x1, Pallas kernels, body(): pl.pallas_call(prepare, out_shape=(pltpu.VMEM((height, rows), jnp.float32...  1.58 us
    pallas_call x1, Pallas kernels, body(): pl.pallas_call(pack, out_shape=pltpu.VMEM((size * LINES, LANES), jnp.bflo...  1.25 us
    pallas_call x1, Pallas kernels, body(): pl.pallas_call(finish, out_shape=jax.ShapeDtypeStruct((picks // size, hei...  0.91 us
  transfers between devices with their start and end apart: 1, of which 1 were waited for; matrix products, arithmetic and copies ran while one was open for 0% of the time, Pallas kernels for 4%

profile of v2, /device:TPU:8, one launch (start us, length us, event | category | flops | bytes accessed | tf_op | source)
XLA Modules:
  0.0 43.3 jit_solution(13429368699375901109)
XLA Ops:
  0.0 1.9 %collective-permute-start = (bf16[512,384]{1,0:T(8,128)(2,1)}, bf16[512,384]{1,0:T(8,128)(2,1)S(1)}, u32[]{:S(2)}, u32[]{:S(2)}) collective-permute-start(bf16[512,384]{1,0:T(8,128)(2,1)} %corpus_ref.1), channel_id=1, source_target_pairs={{0,1},{1,0},{2,3},{3,2},{4,5},{5,4},{6,7},{7,6},{8,9},{9,8},{10,11... | collective-permute-start | bytes 1179656 | tf_op jit(solution)/shard_map/ppermute | solution.py:126
  1.9 1.6 %prepare.1 = (f32[64,512]{1,0:T(8,128)S(1)}, bf16[64,384]{1,0:T(8,128)(2,1)S(1)}, s32[64,1024]{1,0:T(8,128)S(1)}, s32[2,128]{1,0:T(2,128)S(1)}) custom-call(bf16[64,768]{1,0:T(8,128)(2,1)} %queries_ref.1, bf16[512,384]{1,0:T(8,128)(2,1)} %corpus_ref.1, s32[64,1024]{1,0:T(8,128)} %candidates_ref.1), custom_call_target="tpu_custom_call" | custom-call | flops 25165824 | bytes 393216 | tf_op jit(solution)/shard_map/prepare/pallas_call | solution.py:127
  3.5 0.3 collective-permute-done.other_ref
  3.8 1.2 %pack.1 = bf16[1024,128]{1,0:T(8,128)(2,1)S(1)} custom-call(bf16[64,384]{1,0:T(8,128)(2,1)S(1)} %get-tuple-element.9.theirs_ref, bf16[512,384]{1,0:T(8,128)(2,1)S(1)} %collective-permute-done.other_ref, f32[64,512]{1,0:T(8,128)S(1)} %get-tuple-element.10.partial_ref, s32[64,1024]{1,0:T(8,128)S(1)} %get-tuple-element.11.local_ref), custom_call_target="tpu_custom_call" | custom-call | tf_op jit(solution)/shard_map/pack/pallas_call | solution.py:140
  5.1 37.3 %all_to_all.5 = bf16[256,4,128]{2,1,0:T(4,128)(2,1)S(1)} all-to-all(bf16[256,4,128]{2,1,0:T(4,128)(2,1)S(1)} %bitcast.4), channel_id=1, replica_groups=mesh['corpus_0'=8,'corpus_1'=8,'corpus_2'=4,'dim'=2] {'corpus_0','corpus..., dimensions={0} | all-to-all | bytes 524288 | tf_op jit(solution)/shard_map/all_to_all | solution.py:148
  42.4 0.9 %finish.1 = f32[4,64]{1,0:T(4,128)} custom-call(bf16[1024,128]{1,0:T(8,128)(2,1)S(1)} %bitcast.3, s32[2,128]{1,0:T(2,128)S(1)} %get-tuple-element.12.owner_ref), custom_call_target="tpu_custom_call" | custom-call | tf_op jit(solution)/shard_map/finish/pallas_call | solution.py:149
Async XLA Ops:
  0.0 3.8 %collective-permute-start = (bf16[512,384]{1,0:T(8,128)(2,1)}, bf16[512,384]{1,0:T(8,128)(2,1)S(1)}, u32[]{:S(2)}, u32[]{:S(2)}) collective-permute-start(bf16[512,384]{1,0:T(8,128)(2,1)} %corpus_ref.1), channel_id=1, source_target_pairs={{0,1},{1,0},{2,3},{3,2},{4,5},{5,4},{6,7},{7,6},{8,9},{9,8},{10,11... | collective-permute-start | bytes 1179656 | tf_op jit(solution)/shard_map/ppermute | solution.py:126

commit v3 on v2

--- a/solution.py
+++ b/solution.py
@@ -1,3 +1,5 @@
+import functools
+
 import jax
 import jax.numpy as jnp
 from jax import lax
@@ -10,6 +12,14 @@
 LANES = 128
 HALF = LANES // 2
 LINES = 4
+FIRST = (4, 4, 2)
+
+
+def first_rank(shape):
+    position = 0
+    for at, size in zip(FIRST, shape):
+        position = position * size + at
+    return position
 
 
 def lane_gather(table, lanes):
@@ -34,13 +44,13 @@
     return value.astype(jnp.bfloat16).astype(jnp.float32)
 
 
-def prepare(queries_ref, corpus_ref, candidates_ref, partial_ref, theirs_ref, local_ref, owner_ref):
+def prepare(first, queries_ref, corpus_ref, candidates_ref, partial_ref, theirs_ref, local_ref, owner_ref):
     mine, theirs_ref[...] = halves(queries_ref[...], lax.axis_index("dim"))
     partial_ref[...] = matmul_nt(mine, corpus_ref[...])
     height = candidates_ref.shape[0]
     rows = corpus_ref.shape[0]
     position = lax.axis_index(CORPUS)
-    lane = lax.broadcasted_iota(jnp.int32, (height, LANES), 1)
+    lane = lax.broadcasted_iota(jnp.int32, (height, LANES), 1) ^ (first % LANES)
     group = LANES // 4
     quarter = lane // group
     for slot in range(4):
@@ -48,14 +58,14 @@
         for part in range(2):
             value = jnp.zeros((height, LANES), jnp.int32)
             for w in range(4):
-                block = candidates_ref[:, pl.ds((4 * part + w) * LANES, LANES)]
+                block = candidates_ref[:, pl.ds((4 * (part ^ (first // LANES)) + w) * LANES, LANES)]
                 value = jnp.where(quarter == w, lane_gather(block, source), value)
             local_ref[:, pl.ds((2 * slot + part) * LANES, LANES)] = value - position * rows
     own = candidates_ref[:, pl.ds(pl.multiple_of(position // group * LANES, LANES), LANES)]
     at = jnp.full((height, LANES), 4 * (position % group), jnp.int32)
     for pair in range(2):
         both = jnp.concatenate([lane_gather(own, at + 2 * pair), lane_gather(own, at + 2 * pair + 1)], axis=0)
-        owner_ref[pair : pair + 1, :] = (both.astype(jnp.float32).T)[:1, :].astype(jnp.int32) // rows
+        owner_ref[pair : pair + 1, :] = ((both.astype(jnp.float32).T)[:1, :].astype(jnp.int32) // rows) ^ first
 
 
 def pack(theirs_ref, other_ref, partial_ref, local_ref, out_ref, lines_ref):
@@ -123,9 +133,10 @@
     rows, width = corpus.shape
     height, picks = candidates.shape
     size = lax.axis_size(CORPUS)
+    first = first_rank([lax.axis_size(axis) for axis in CORPUS])
     other = lax.ppermute(corpus, "dim", [(0, 1), (1, 0)])
     partial, theirs, local, owner = pl.pallas_call(
-        prepare,
+        functools.partial(prepare, first),
         out_shape=(
             pltpu.VMEM((height, rows), jnp.float32),
             pltpu.VMEM((height, width), queries.dtype),
@@ -145,7 +156,10 @@
         scratch_shapes=[pltpu.VMEM((size * LINES, LANES), jnp.float32)],
         name="pack",
     )(on_chip(theirs), on_chip(other), on_chip(partial), on_chip(local))
-    arrived = lax.all_to_all(sent.reshape(size, LINES, LANES), CORPUS, split_axis=0, concat_axis=0, tiled=True)
+    ranks = [[rank ^ first for rank in range(size)]]
+    arrived = lax.all_to_all(
+        sent.reshape(size, LINES, LANES), CORPUS, split_axis=0, concat_axis=0, axis_index_groups=ranks, tiled=True
+    )
     out = pl.pallas_call(
         finish,
         out_shape=jax.ShapeDtypeStruct((picks // size, height), jnp.float32),

time: 43.5 us -> 37.6 us (0.86)
  the two profiles are of different devices: /device:TPU:8 before, /device:TPU:1 now
where the time goes in v3:
time: 37.6 us; the launch traced here: 37.4 us
  blocking collectives  24.9 us (66%)
  starting transfers between devices  8.73 us (23%)
  Pallas kernels  3.74 us (10%)
    all_to_all x1, blocking collectives, body(): lax.all_to_all(sent.reshape(size, LINES, LANES), CORPUS, split_axis=0, co...  24.9 us
    ppermute x1, starting transfers between devices, body(): other = lax.ppermute(corpus, 'dim', [(0, 1), (1, 0)])  8.73 us
    pallas_call x1, Pallas kernels, body(): pl.pallas_call(functools.partial(prepare, first), out_shape=(pltpu.VMEM((...  1.58 us
    pallas_call x1, Pallas kernels, body(): pl.pallas_call(pack, out_shape=pltpu.VMEM((size * LINES, LANES), jnp.bflo...  1.25 us
    pallas_call x1, Pallas kernels, body(): pl.pallas_call(finish, out_shape=jax.ShapeDtypeStruct((picks // size, hei...  0.91 us
  transfers between devices with their start and end apart: 1, of which 0 were waited for; matrix products, arithmetic and copies ran while one was open for 0% of the time, Pallas kernels for 4%

profile of v3, /device:TPU:1, one launch (start us, length us, event | category | flops | bytes accessed | tf_op | source)
XLA Modules:
  0.0 37.4 jit_solution(12913044718173376485)
XLA Ops:
  0.0 8.7 %collective-permute-start = (bf16[512,384]{1,0:T(8,128)(2,1)}, bf16[512,384]{1,0:T(8,128)(2,1)S(1)}, u32[]{:S(2)}, u32[]{:S(2)}) collective-permute-start(bf16[512,384]{1,0:T(8,128)(2,1)} %corpus_ref.1), channel_id=1, source_target_pairs={{0,1},{1,0},{2,3},{3,2},{4,5},{5,4},{6,7},{7,6},{8,9},{9,8},{10,11... | collective-permute-start | bytes 1179656 | tf_op jit(solution)/shard_map/ppermute | solution.py:137
  8.7 1.6 %prepare.1 = (f32[64,512]{1,0:T(8,128)S(1)}, bf16[64,384]{1,0:T(8,128)(2,1)S(1)}, s32[64,1024]{1,0:T(8,128)S(1)}, s32[2,128]{1,0:T(2,128)S(1)}) custom-call(bf16[64,768]{1,0:T(8,128)(2,1)} %queries_ref.1, bf16[512,384]{1,0:T(8,128)(2,1)} %corpus_ref.1, s32[64,1024]{1,0:T(8,128)} %candidates_ref.1), custom_call_target="tpu_custom_call" | custom-call | flops 25165824 | bytes 393216 | tf_op jit(solution)/shard_map/prepare/pallas_call | solution.py:138
  10.3 0.0 collective-permute-done.other_ref
  10.3 1.2 %pack.1 = bf16[1024,128]{1,0:T(8,128)(2,1)S(1)} custom-call(bf16[64,384]{1,0:T(8,128)(2,1)S(1)} %get-tuple-element.9.theirs_ref, bf16[512,384]{1,0:T(8,128)(2,1)S(1)} %collective-permute-done.other_ref, f32[64,512]{1,0:T(8,128)S(1)} %get-tuple-element.10.partial_ref, s32[64,1024]{1,0:T(8,128)S(1)} %get-tuple-element.11.local_ref), custom_call_target="tpu_custom_call" | custom-call | tf_op jit(solution)/shard_map/pack/pallas_call | solution.py:151
  11.6 24.9 %all_to_all.5 = bf16[256,4,128]{2,1,0:T(4,128)(2,1)S(1)} all-to-all(bf16[256,4,128]{2,1,0:T(4,128)(2,1)S(1)} %bitcast.4), channel_id=1, replica_groups={{292,294,288,290,300,302,296,298,308,310,304,306,316,318,312,314,260,26..., dimensions={0} | all-to-all | bytes 524288 | tf_op jit(solution)/shard_map/all_to_all | solution.py:160
  36.5 0.9 %finish.1 = f32[4,64]{1,0:T(4,128)} custom-call(bf16[1024,128]{1,0:T(8,128)(2,1)S(1)} %bitcast.3, s32[2,128]{1,0:T(2,128)S(1)} %get-tuple-element.12.owner_ref), custom_call_target="tpu_custom_call" | custom-call | tf_op jit(solution)/shard_map/finish/pallas_call | solution.py:163
Async XLA Ops:
  0.0 10.3 %collective-permute-start = (bf16[512,384]{1,0:T(8,128)(2,1)}, bf16[512,384]{1,0:T(8,128)(2,1)S(1)}, u32[]{:S(2)}, u32[]{:S(2)}) collective-permute-start(bf16[512,384]{1,0:T(8,128)(2,1)} %corpus_ref.1), channel_id=1, source_target_pairs={{0,1},{1,0},{2,3},{3,2},{4,5},{5,4},{6,7},{7,6},{8,9},{9,8},{10,11... | collective-permute-start | bytes 1179656 | tf_op jit(solution)/shard_map/ppermute | solution.py:137

commit v4 on v3

v4 whole, which is shorter than its diff:
```python
import functools

import jax
import jax.numpy as jnp
from jax import lax
from jax.experimental import pallas as pl
from jax.experimental.pallas import tpu as pltpu
from jax.sharding import Mesh
from jax.sharding import PartitionSpec as P

CORPUS = ("corpus_0", "corpus_1", "corpus_2")
LANES = 128
HALF = LANES // 2
GROUP = LANES // 4
LINES = 4
FIRST = (4, 4, 2)


def first_rank(shape):
    position = 0
    for at, size in zip(FIRST, shape):
        position = position * size + at
    return position


def lane_gather(table, lanes):
    numbers = lax.GatherDimensionNumbers(
        offset_dims=(),
        collapsed_slice_dims=(1,),
        start_index_map=(1,),
        operand_batching_dims=(0,),
        start_indices_batching_dims=(0,),
    )
    return lax.gather(
        table, lanes[:, :, None], numbers, slice_sizes=(1, 1), mode=lax.GatherScatterMode.PROMISE_IN_BOUNDS
    )


def halves(queries, dim):
    half = queries.shape[1] // 2
    first, second = queries[:, :half], queries[:, half:]
    return jnp.where(dim == 0, first, second), jnp.where(dim == 0, second, first)


def matmul_nt(left, right):
    return lax.dot_general(left, right, (((1,), (1,)), ((), ())), preferred_element_type=jnp.float32)


def rounded(value):
    return value.astype(jnp.bfloat16).astype(jnp.float32)


def prepare(
    first,
    queries_in,
    corpus_in,
    candidates_in,
    partial_ref,
    theirs_ref,
    local_ref,
    owner_ref,
    order_ref,
    queries_ref,
    corpus_ref,
    candidates_ref,
    arrived,
):
    loads = [
        pltpu.make_async_copy(source, target, arrived.at[k])
        for k, (source, target) in enumerate(
            [(candidates_in, candidates_ref), (queries_in, queries_ref), (corpus_in, corpus_ref)]
        )
    ]
    for load in loads:
        load.start()
    row = lax.broadcasted_iota(jnp.int32, (2 * LANES, 1), 0)
    line = row % LINES
    taken = jnp.where(line < 2, row // LANES * HALF + line * GROUP + row % LANES // LINES, LANES + (line - 2) * HALF)
    column = lax.broadcasted_iota(jnp.int32, (2 * LANES, 2 * LANES), 1)
    order_ref[...] = jnp.where(column == taken, 1.0, 0.0).astype(jnp.bfloat16)
    height = candidates_ref.shape[0]
    rows = corpus_ref.shape[0]
    position = lax.axis_index(CORPUS)
    lane = lax.broadcasted_iota(jnp.int32, (height, LANES), 1)
    loads[0].wait()
    for side in range(2):
        source = 4 * ((lane % GROUP) ^ (first % GROUP)) + 2 * (lane % HALF // GROUP) + side
        for pair in range(4):
            low, high = [
                lane_gather(candidates_ref[:, pl.ds(((2 * pair + k) ^ (first // GROUP)) * LANES, LANES)], source)
                for k in range(2)
            ]
            local_ref[:, pl.ds((2 * pair + side) * LANES, LANES)] = jnp.where(lane < HALF, low, high) - position * rows
    own = candidates_ref[:, pl.ds(pl.multiple_of(position // GROUP * LANES, LANES), LANES)]
    at = jnp.full((height, LANES), 4 * (position % GROUP), jnp.int32)
    for line in range(2):
        both = jnp.concatenate([lane_gather(own, at + 2 * line), lane_gather(own, at + 2 * line + 1)], axis=0)
        owner_ref[line : line + 1, :] = ((both.astype(jnp.float32).T)[:1, :].astype(jnp.int32) // rows) ^ first
    loads[1].wait()
    mine, theirs_ref[...] = halves(queries_ref[...], lax.axis_index("dim"))
    loads[2].wait()
    partial_ref[...] = matmul_nt(mine, corpus_ref[...])


def pack(theirs_ref, other_ref, partial_ref, local_ref, order_ref, out_ref):
    scores = partial_ref[...] + matmul_nt(theirs_ref[...], other_ref[...])
    height, count = scores.shape
    peak = jnp.max(scores, axis=1, keepdims=True)
    lse = peak + jnp.log(jnp.sum(jnp.exp(scores - peak), axis=1, keepdims=True))
    center = rounded(jnp.sum(scores, axis=1, keepdims=True) * (1.0 / count))
    moved = scores - center
    upper = rounded(lse)
    middle = rounded(lse - upper)
    lower = lse - upper - middle
    low = lax.broadcasted_iota(jnp.int32, (height, LANES), 1) < HALF
    stats = jnp.concatenate([jnp.where(low, upper, lower), jnp.where(low, middle, center)], axis=0).astype(jnp.bfloat16)

    blocks = count // LANES
    parts = [[] for _ in range(8)]
    for top in range(0, height, 8):
        for column in range(8):
            local = local_ref[top : top + 8, pl.ds(column * LANES, LANES)]
            block, lane = local >> 7, local & (LANES - 1)
            value = jnp.zeros((8, LANES), jnp.float32)
            for w in range(blocks):
                table = moved[top : top + 8, w * LANES : (w + 1) * LANES]
                value = jnp.where(block == w, lane_gather(table, lane), value)
            parts[column].append(value)
    picked = [jnp.concatenate(part, axis=0) for part in parts]
    for pair in range(4):
        both = jnp.concatenate([picked[2 * pair], picked[2 * pair + 1]], axis=0).astype(jnp.bfloat16)
        lines = matmul_nt(order_ref[...], jnp.concatenate([both, stats], axis=1))
        out_ref[pl.ds(2 * LANES * pair, 2 * LANES), :] = lines.astype(jnp.bfloat16)


def finish(all_ref, owner_ref, out_ref, lines_ref):
    lines_ref[...] = all_ref[...].astype(jnp.float32)
    sources = all_ref.shape[0] // LINES
    first = lines_ref[pl.ds(2, sources, stride=LINES), :]
    second = lines_ref[pl.ds(3, sources, stride=LINES), :]
    local = first + pltpu.roll(first, HALF, 1) + second
    low = lax.broadcasted_iota(jnp.int32, (1, LANES), 1) < HALF
    peak = jnp.max(local, axis=0, keepdims=True)
    mass = jnp.sum(jnp.exp(local - peak), axis=0, keepdims=True)
    lse = (peak + jnp.log(mass))[:, :HALF]
    center = jnp.where(low, pltpu.roll(second, HALF, 1), second)
    source = lax.broadcasted_iota(jnp.int32, (sources, LANES), 0)
    for pair in range(2):
        moved = lines_ref[pl.ds(pair, sources, stride=LINES), :]
        back = jnp.where(source == owner_ref[pair : pair + 1, :], center, 0.0)
        picked = jnp.sum(moved + back, axis=0, keepdims=True)
        out_ref[2 * pair : 2 * pair + 1, :] = picked[:, :HALF] - lse
        out_ref[2 * pair + 1 : 2 * pair + 2, :] = picked[:, HALF:] - lse


VMEM = pl.BlockSpec(memory_space=pltpu.VMEM)
ANY = pl.BlockSpec(memory_space=pl.ANY)


def on_chip(value):
    return pltpu.with_memory_space_constraint(value, pltpu.VMEM)


def body(queries, corpus, candidates):
    rows, width = corpus.shape
    height, picks = candidates.shape
    size = lax.axis_size(CORPUS)
    first = first_rank([lax.axis_size(axis) for axis in CORPUS])
    other = lax.ppermute(corpus, "dim", [(0, 1), (1, 0)])
    partial, theirs, local, owner, order = pl.pallas_call(
        functools.partial(prepare, first),
        out_shape=(
            pltpu.VMEM((height, rows), jnp.float32),
            pltpu.VMEM((height, width), queries.dtype),
            pltpu.VMEM((height, picks), jnp.int32),
            pltpu.VMEM((2, LANES), jnp.int32),
            pltpu.VMEM((2 * LANES, 2 * LANES), jnp.bfloat16),
        ),
        in_specs=[ANY, ANY, ANY],
        out_specs=(VMEM, VMEM, VMEM, VMEM, VMEM),
        scratch_shapes=[
            pltpu.VMEM(queries.shape, queries.dtype),
            pltpu.VMEM(corpus.shape, corpus.dtype),
            pltpu.VMEM(candidates.shape, candidates.dtype),
            pltpu.SemaphoreType.DMA((3,)),
        ],
        cost_estimate=pl.CostEstimate(flops=2 * height * rows * width, bytes_accessed=2 * rows * width, transcendentals=0),
        name="prepare",
    )(queries, corpus, candidates)
    sent = pl.pallas_call(
        pack,
        out_shape=pltpu.VMEM((size * LINES, LANES), jnp.bfloat16),
        in_specs=[VMEM, VMEM, VMEM, VMEM, VMEM],
        out_specs=VMEM,
        name="pack",
    )(on_chip(theirs), on_chip(other), on_chip(partial), on_chip(local), on_chip(order))
    ranks = [[rank ^ first for rank in range(size)]]
    arrived = lax.all_to_all(
        sent.reshape(size, LINES, LANES), CORPUS, split_axis=0, concat_axis=0, axis_index_groups=ranks, tiled=True
    )
    out = pl.pallas_call(
        finish,
        out_shape=jax.ShapeDtypeStruct((picks // size, height), jnp.float32),
        in_specs=[VMEM, VMEM],
        out_specs=VMEM,
        scratch_shapes=[pltpu.VMEM((size * LINES, LANES), jnp.float32)],
        name="finish",
    )(on_chip(arrived.reshape(size * LINES, LANES)), on_chip(owner))
    return out.T


def solution(mesh):
    torus = Mesh(
        mesh.devices.reshape(8, 8, 4, mesh.shape["dim"]),
        (*CORPUS, "dim"),
    )
    return jax.shard_map(
        body,
        mesh=torus,
        in_specs=(P("dim", None), P(CORPUS, "dim"), P("dim", None)),
        out_specs=P("dim", CORPUS),
        check_vma=False,
    )
```

time: 37.6 us -> 37.4 us (level)
  no operation moved by 1% of the time
where the time goes in v4:
time: 37.4 us; the launch traced here: 37.2 us
  blocking collectives  24.9 us (67%)
  starting transfers between devices  8.73 us (23%)
  Pallas kernels  3.53 us (9%)
    all_to_all x1, blocking collectives, body(): lax.all_to_all(sent.reshape(size, LINES, LANES), CORPUS, split_axis=0, co...  24.9 us
    ppermute x1, starting transfers between devices, body(): other = lax.ppermute(corpus, 'dim', [(0, 1), (1, 0)])  8.73 us
    pallas_call x1, Pallas kernels, body(): pl.pallas_call(functools.partial(prepare, first), out_shape=(pltpu.VMEM((...  1.55 us
    pallas_call x1, Pallas kernels, body(): pl.pallas_call(pack, out_shape=pltpu.VMEM((size * LINES, LANES), jnp.bflo...  1.07 us
    pallas_call x1, Pallas kernels, body(): pl.pallas_call(finish, out_shape=jax.ShapeDtypeStruct((picks // size, hei...  0.91 us
  transfers between devices with their start and end apart: 1, of which 0 were waited for; matrix products, arithmetic and copies ran while one was open for 0% of the time, Pallas kernels for 4%

profile of v4, /device:TPU:1, one launch (start us, length us, event | category | flops | bytes accessed | tf_op | source)
XLA Modules:
  0.0 37.2 jit_solution(17807679798493085277)
XLA Ops:
  0.0 8.7 %collective-permute-start = (bf16[512,384]{1,0:T(8,128)(2,1)}, bf16[512,384]{1,0:T(8,128)(2,1)S(1)}, u32[]{:S(2)}, u32[]{:S(2)}) collective-permute-start(bf16[512,384]{1,0:T(8,128)(2,1)} %corpus_in.1), channel_id=1, source_target_pairs={{0,1},{1,0},{2,3},{3,2},{4,5},{5,4},{6,7},{7,6},{8,9},{9,8},{10,11... | collective-permute-start | bytes 1179656 | tf_op jit(solution)/shard_map/ppermute | solution.py:169
  8.7 1.5 %prepare.1 = (f32[64,512]{1,0:T(8,128)S(1)}, bf16[64,384]{1,0:T(8,128)(2,1)S(1)}, s32[64,1024]{1,0:T(8,128)S(1)}, s32[2,128]{1,0:T(2,128)S(1)}, bf16[256,256]{1,0:T(8,128)(2,1)S(1)}) custom-call(bf16[64,768]{1,0:T(8,128)(2,1)} %queries_in.1, bf16[512,384]{1,0:T(8,128)(2,1)} %corpus_in.1, s32[64,1024]{1,0:T(8,128)} %candidates_in.1), custom_call_target="tpu_custom_call" | custom-call | flops 25165824 | bytes 393216 | tf_op jit(solution)/shard_map/prepare/pallas_call | solution.py:170
  10.3 0.0 collective-permute-done.other_ref
  10.3 1.1 %pack.1 = bf16[1024,128]{1,0:T(8,128)(2,1)S(1)} custom-call(bf16[64,384]{1,0:T(8,128)(2,1)S(1)} %get-tuple-element.10.theirs_ref, bf16[512,384]{1,0:T(8,128)(2,1)S(1)} %collective-permute-done.other_ref, f32[64,512]{1,0:T(8,128)S(1)} %get-tuple-element.11.partial_ref, s32[64,1024]{1,0:T(8,128)S(1)} %get-tuple-element.12.local_ref, ...), custom_call_target="tpu_custom_call" | custom-call | tf_op jit(solution)/shard_map/pack/pallas_call | solution.py:190
  11.4 24.9 %all_to_all.5 = bf16[256,4,128]{2,1,0:T(4,128)(2,1)S(1)} all-to-all(bf16[256,4,128]{2,1,0:T(4,128)(2,1)S(1)} %bitcast.3), channel_id=1, replica_groups={{292,294,288,290,300,302,296,298,308,310,304,306,316,318,312,314,260,26..., dimensions={0} | all-to-all | bytes 524288 | tf_op jit(solution)/shard_map/all_to_all | solution.py:198
  36.3 0.9 %finish.1 = f32[4,64]{1,0:T(4,128)} custom-call(bf16[1024,128]{1,0:T(8,128)(2,1)S(1)} %bitcast.4, s32[2,128]{1,0:T(2,128)S(1)} %get-tuple-element.14.owner_ref), custom_call_target="tpu_custom_call" | custom-call | tf_op jit(solution)/shard_map/finish/pallas_call | solution.py:201
Async XLA Ops:
  0.0 10.3 %collective-permute-start = (bf16[512,384]{1,0:T(8,128)(2,1)}, bf16[512,384]{1,0:T(8,128)(2,1)S(1)}, u32[]{:S(2)}, u32[]{:S(2)}) collective-permute-start(bf16[512,384]{1,0:T(8,128)(2,1)} %corpus_in.1), channel_id=1, source_target_pairs={{0,1},{1,0},{2,3},{3,2},{4,5},{5,4},{6,7},{7,6},{8,9},{9,8},{10,11... | collective-permute-start | bytes 1179656 | tf_op jit(solution)/shard_map/ppermute | solution.py:169

commit v5 on v3

v5 whole, which is shorter than its diff:
```python
import functools

import jax
import jax.numpy as jnp
from jax import lax
from jax.experimental import pallas as pl
from jax.experimental.pallas import tpu as pltpu
from jax.sharding import Mesh
from jax.sharding import PartitionSpec as P

CORPUS = ("corpus_0", "corpus_1", "corpus_2")
LANES = 128
HALF = LANES // 2
GROUP = LANES // 4
LINES = 4
TINY = 1e-30
FIRST = (4, 4, 2)


def first_rank(shape):
    position = 0
    for at, size in zip(FIRST, shape):
        position = position * size + at
    return position


def lane_gather(table, lanes):
    numbers = lax.GatherDimensionNumbers(
        offset_dims=(),
        collapsed_slice_dims=(1,),
        start_index_map=(1,),
        operand_batching_dims=(0,),
        start_indices_batching_dims=(0,),
    )
    return lax.gather(
        table, lanes[:, :, None], numbers, slice_sizes=(1, 1), mode=lax.GatherScatterMode.PROMISE_IN_BOUNDS
    )


def matmul_nt(left, right):
    return lax.dot_general(left, right, (((1,), (1,)), ((), ())), preferred_element_type=jnp.float32)


def rounded(value):
    return value.astype(jnp.bfloat16).astype(jnp.float32)


def message_order(first):
    row = lax.broadcasted_iota(jnp.int32, (LANES, LANES), 0)
    lane = lax.broadcasted_iota(jnp.int32, (LANES, LANES), 1)
    line = row % LINES
    slot = LINES * (row // LINES ^ (first % GROUP)) + 2 * line
    picks = line < 2
    hits = [picks & (lane == slot), picks & (lane == slot + 1), lane == (line - 2) * HALF]
    return jnp.concatenate([jnp.where(hit, 1.0, 0.0).astype(jnp.bfloat16) for hit in hits], axis=1)


def pack(first, queries_ref, corpus_ref, candidates_ref, out_ref):
    width = corpus_ref.shape[2]
    scores = matmul_nt(queries_ref[:, :width], corpus_ref[0]) + matmul_nt(queries_ref[:, width:], corpus_ref[1])
    height, count = scores.shape
    order = message_order(first)
    peak = jnp.max(scores, axis=1, keepdims=True)
    lse = peak + jnp.log(jnp.sum(jnp.exp(scores - peak), axis=1, keepdims=True))
    center = rounded(jnp.sum(scores, axis=1, keepdims=True) * (1.0 / count))
    moved = scores - center
    moved = jnp.where(jnp.abs(moved) < TINY, TINY, moved)
    upper = rounded(lse)
    middle = rounded(lse - upper)
    lower = lse - upper - middle
    low = lax.broadcasted_iota(jnp.int32, (height, LANES), 1) < HALF
    stats = jnp.concatenate([jnp.where(low, upper, lower), jnp.where(low, middle, center)], axis=0).astype(jnp.bfloat16)
    offset = lax.axis_index(CORPUS) * count
    nothing = jnp.zeros((height, LANES), jnp.bfloat16)
    for tile in range(candidates_ref.shape[1] // LANES):
        local = candidates_ref[:, tile * LANES : (tile + 1) * LANES] - offset
        block, lane = local >> 7, local & (LANES - 1)
        value = jnp.zeros((height, LANES), jnp.float32)
        for w in range(count // LANES):
            value = jnp.where(block == w, lane_gather(moved[:, w * LANES : (w + 1) * LANES], lane), value)
        value = value.astype(jnp.bfloat16)
        both = jnp.concatenate(
            [jnp.concatenate([value, nothing], axis=0), jnp.concatenate([nothing, value], axis=0), stats], axis=1
        )
        group = tile ^ (first // GROUP)
        out_ref[group * LANES : (group + 1) * LANES, :] = matmul_nt(order, both).astype(jnp.bfloat16)


def finish(all_ref, out_ref, lines_ref):
    lines_ref[...] = all_ref[...].astype(jnp.float32)
    sources = all_ref.shape[0] // LINES
    first = lines_ref[pl.ds(2, sources, stride=LINES), :]
    second = lines_ref[pl.ds(3, sources, stride=LINES), :]
    local = first + pltpu.roll(first, HALF, 1) + second
    low = lax.broadcasted_iota(jnp.int32, (1, LANES), 1) < HALF
    peak = jnp.max(local, axis=0, keepdims=True)
    mass = jnp.sum(jnp.exp(local - peak), axis=0, keepdims=True)
    lse = (peak + jnp.log(mass))[:, :HALF]
    center = jnp.where(low, pltpu.roll(second, HALF, 1), second)
    for pair in range(2):
        moved = lines_ref[pl.ds(pair, sources, stride=LINES), :]
        picked = jnp.sum(jnp.where(moved != 0.0, moved + center, 0.0), axis=0, keepdims=True)
        out_ref[2 * pair : 2 * pair + 1, :] = picked[:, :HALF] - lse
        out_ref[2 * pair + 1 : 2 * pair + 2, :] = picked[:, HALF:] - lse


VMEM = pl.BlockSpec(memory_space=pltpu.VMEM)


def on_chip(value):
    return pltpu.with_memory_space_constraint(value, pltpu.VMEM)


def body(queries, corpus, candidates):
    height, picks = candidates.shape
    size = lax.axis_size(CORPUS)
    first = first_rank([lax.axis_size(axis) for axis in CORPUS])
    both = lax.all_gather(corpus, "dim")
    sent = pl.pallas_call(
        functools.partial(pack, first),
        out_shape=pltpu.VMEM((size * LINES, LANES), jnp.bfloat16),
        in_specs=[VMEM, VMEM, VMEM],
        out_specs=VMEM,
        name="pack",
    )(on_chip(queries), on_chip(both), on_chip(candidates))
    ranks = [[rank ^ first for rank in range(size)]]
    arrived = lax.all_to_all(
        sent.reshape(size, LINES, LANES), CORPUS, split_axis=0, concat_axis=0, axis_index_groups=ranks, tiled=True
    )
    out = pl.pallas_call(
        finish,
        out_shape=jax.ShapeDtypeStruct((picks // size, height), jnp.float32),
        in_specs=[VMEM],
        out_specs=VMEM,
        scratch_shapes=[pltpu.VMEM((size * LINES, LANES), jnp.float32)],
        name="finish",
    )(on_chip(arrived.reshape(size * LINES, LANES)))
    return out.T


def solution(mesh):
    torus = Mesh(
        mesh.devices.reshape(8, 8, 4, mesh.shape["dim"]),
        (*CORPUS, "dim"),
    )
    return jax.shard_map(
        body,
        mesh=torus,
        in_specs=(P("dim", None), P(CORPUS, "dim"), P("dim", None)),
        out_specs=P("dim", CORPUS),
        check_vma=False,
    )
```

time: 37.6 us -> 36.3 us (0.965)
  blocking collectives: 24.9 us -> 34 us
  starting transfers between devices: 8.73 us -> 0 us
  Pallas kernels: 3.74 us -> 2.13 us
    all_gather x0 -> x1, blocking collectives: none -> 9.16 us  [body(): both = lax.all_gather(corpus, 'dim')]
    ppermute x1 -> x0, starting transfers between devices: 8.73 us -> none  [body(): other = lax.ppermute(corpus, 'dim', [(0, 1), (1, 0)])]
    pallas_call x2 -> x1, Pallas kernels: 2.83 us -> 1.22 us  [body(): pl.pallas_call(functools.partial(pack, first), out_shape=pltpu.VMEM((size...]
  transfers between devices with their start and end apart: 1 -> 0, of which waited for: 0 -> 0; matrix products, arithmetic and copies ran while one was open for 0% -> 0% of each run, Pallas kernels for 4% -> 0%
where the time goes in v5:
time: 36.3 us; the launch traced here: 36.1 us
  blocking collectives  34 us (94%)
  Pallas kernels  2.13 us (6%)
    all_to_all x1, blocking collectives, body(): lax.all_to_all(sent.reshape(size, LINES, LANES), CORPUS, split_axis=0, co...  24.8 us
    all_gather x1, blocking collectives, body(): both = lax.all_gather(corpus, 'dim')  9.16 us
    pallas_call x1, Pallas kernels, body(): pl.pallas_call(functools.partial(pack, first), out_shape=pltpu.VMEM((size...  1.22 us
    pallas_call x1, Pallas kernels, body(): pl.pallas_call(finish, out_shape=jax.ShapeDtypeStruct((picks // size, hei...  0.91 us

profile of v5, /device:TPU:1, one launch (start us, length us, event | category | flops | bytes accessed | tf_op | source)
XLA Modules:
  0.0 36.1 jit_solution(11371498015926458660)
XLA Ops:
  0.0 0.0 copy-start
  0.0 0.0 copy-start.1
  0.0 9.2 %all-gather = bf16[1024,384]{1,0:T(8,128)(2,1)S(1)} all-gather(bf16[512,384]{1,0:T(8,128)(2,1)} %param.4), channel_id=2, replica_groups=mesh['corpus_0'=8,'corpus_1'=8,'corpus_2'=4,'dim'=2] {'dim'}, dimensions={0}, use_global_device_ids=true | all-gather | bytes 1179648 | tf_op jit(solution)/shard_map/all_gather | solution.py:118
  9.2 0.0 copy-done
  9.2 0.0 copy-done.1
  9.2 1.2 %pack.1 = bf16[1024,128]{1,0:T(8,128)(2,1)S(1)} custom-call(bf16[64,768]{1,0:T(8,128)(2,1)S(1)} %copy-done.1, bf16[2,512,384]{2,1,0:T(8,128)(2,1)S(1)} %bitcast.4, s32[64,1024]{1,0:T(8,128)S(1)} %copy-done), custom_call_target="tpu_custom_call" | custom-call | tf_op jit(solution)/shard_map/pack/pallas_call | solution.py:119
  10.4 24.8 %all_to_all.5 = bf16[256,4,128]{2,1,0:T(4,128)(2,1)S(1)} all-to-all(bf16[256,4,128]{2,1,0:T(4,128)(2,1)S(1)} %bitcast.6), channel_id=1, replica_groups={{292,294,288,290,300,302,296,298,308,310,304,306,316,318,312,314,260,26..., dimensions={0} | all-to-all | bytes 524288 | tf_op jit(solution)/shard_map/all_to_all | solution.py:127
  35.2 0.9 %finish.1 = f32[4,64]{1,0:T(4,128)} custom-call(bf16[1024,128]{1,0:T(8,128)(2,1)S(1)} %bitcast.5), custom_call_target="tpu_custom_call" | custom-call | tf_op jit(solution)/shard_map/finish/pallas_call | solution.py:130
Async XLA Ops:
  0.0 9.2 %copy-start = (s32[64,1024]{1,0:T(8,128)S(1)}, s32[64,1024]{1,0:T(8,128)}, u32[]{:S(2)}) copy-start(s32[64,1024]{1,0:T(8,128)} %candidates_ref.1) | copy-start | bytes 786436
  0.0 9.2 %copy-start.1 = (bf16[64,768]{1,0:T(8,128)(2,1)S(1)}, bf16[64,768]{1,0:T(8,128)(2,1)}, u32[]{:S(2)}) copy-start(bf16[64,768]{1,0:T(8,128)(2,1)} %queries_ref.1) | copy-start | bytes 294916

commit v6 on v5

--- a/solution.py
+++ b/solution.py
@@ -11,8 +11,10 @@
 CORPUS = ("corpus_0", "corpus_1", "corpus_2")
 LANES = 128
 HALF = LANES // 2
-GROUP = LANES // 4
 LINES = 4
+RING = 4
+TILE = 16
+MESSAGE = LANES + TILE
 TINY = 1e-30
 FIRST = (4, 4, 2)
 
@@ -41,30 +43,36 @@
     return lax.dot_general(left, right, (((1,), (1,)), ((), ())), preferred_element_type=jnp.float32)
 
 
+def kept_off_zero(value):
+    return jnp.where(jnp.abs(value) < TINY, TINY, value)
+
+
 def rounded(value):
     return value.astype(jnp.bfloat16).astype(jnp.float32)
 
 
-def message_order(first):
-    row = lax.broadcasted_iota(jnp.int32, (LANES, LANES), 0)
-    lane = lax.broadcasted_iota(jnp.int32, (LANES, LANES), 1)
-    line = row % LINES
-    slot = LINES * (row // LINES ^ (first % GROUP)) + 2 * line
-    picks = line < 2
-    hits = [picks & (lane == slot), picks & (lane == slot + 1), lane == (line - 2) * HALF]
-    return jnp.concatenate([jnp.where(hit, 1.0, 0.0).astype(jnp.bfloat16) for hit in hits], axis=1)
+def ones_where(hit):
+    return jnp.where(hit, 1.0, 0.0).astype(jnp.bfloat16)
+
+
+def ring_order(first):
+    row = lax.broadcasted_iota(jnp.int32, (HALF, LANES), 0)
+    lane = lax.broadcasted_iota(jnp.int32, (HALF, LANES), 1)
+    near = row // TILE ^ (first % RING)
+    far = row % TILE // 2 ^ (first // RING % 8)
+    slot = TILE * far + 4 * near + 2 * (row % 2)
+    return jnp.concatenate([ones_where(lane == slot), ones_where(lane == slot + 1)], axis=1)
 
 
 def pack(first, queries_ref, corpus_ref, candidates_ref, out_ref):
     width = corpus_ref.shape[2]
     scores = matmul_nt(queries_ref[:, :width], corpus_ref[0]) + matmul_nt(queries_ref[:, width:], corpus_ref[1])
     height, count = scores.shape
-    order = message_order(first)
+    order = ring_order(first)
     peak = jnp.max(scores, axis=1, keepdims=True)
     lse = peak + jnp.log(jnp.sum(jnp.exp(scores - peak), axis=1, keepdims=True))
     center = rounded(jnp.sum(scores, axis=1, keepdims=True) * (1.0 / count))
-    moved = scores - center
-    moved = jnp.where(jnp.abs(moved) < TINY, TINY, moved)
+    moved = kept_off_zero(scores - center)
     upper = rounded(lse)
     middle = rounded(lse - upper)
     lower = lse - upper - middle
@@ -80,10 +88,47 @@
             value = jnp.where(block == w, lane_gather(moved[:, w * LANES : (w + 1) * LANES], lane), value)
         value = value.astype(jnp.bfloat16)
         both = jnp.concatenate(
-            [jnp.concatenate([value, nothing], axis=0), jnp.concatenate([nothing, value], axis=0), stats], axis=1
+            [jnp.concatenate([value, nothing], axis=0), jnp.concatenate([nothing, value], axis=0)], axis=1
         )
-        group = tile ^ (first // GROUP)
-        out_ref[group * LANES : (group + 1) * LANES, :] = matmul_nt(order, both).astype(jnp.bfloat16)
+        lines = matmul_nt(order, both).astype(jnp.bfloat16)
+        at = TILE * (tile ^ (first // RING // 8))
+        for near in range(RING):
+            out_ref[near * MESSAGE + at : near * MESSAGE + at + TILE, :] = lines[near * TILE : (near + 1) * TILE]
+    row = lax.broadcasted_iota(jnp.int32, (TILE, LANES), 0)
+    lane = lax.broadcasted_iota(jnp.int32, (TILE, LANES), 1)
+    last = matmul_nt(ones_where((row < 2) & (lane == row * HALF)), stats).astype(jnp.bfloat16)
+    for near in range(RING):
+        out_ref[near * MESSAGE + LANES : (near + 1) * MESSAGE, :] = last
+
+
+def merge(ring_ref, out_ref):
+    low = lax.broadcasted_iota(jnp.int32, (1, LANES), 1) < HALF
+    stats = [ring_ref[k * MESSAGE + LANES : (k + 1) * MESSAGE, :].astype(jnp.float32) for k in range(RING)]
+    locals_, centers = [], []
+    for stat in stats:
+        one, two = stat[0:1], stat[1:2]
+        turned = pltpu.roll(two, HALF, 1)
+        locals_.append(one + pltpu.roll(one, HALF, 1) + jnp.where(low, two, turned))
+        centers.append(jnp.where(low, turned, two))
+    peak = functools.reduce(jnp.maximum, locals_)
+    lse = peak + jnp.log(sum(jnp.exp(local - peak) for local in locals_))
+    center = rounded(sum(centers) * (1.0 / RING))
+    picked = jnp.zeros((LANES, LANES), jnp.float32)
+    for k in range(RING):
+        sent = ring_ref[k * MESSAGE : k * MESSAGE + LANES, :].astype(jnp.float32)
+        picked = jnp.where(sent != 0.0, kept_off_zero(sent + (centers[k] - center)), picked)
+    upper = rounded(lse)
+    middle = rounded(lse - upper)
+    lower = lse - upper - middle
+    rows = out_ref.shape[0]
+    row = lax.broadcasted_iota(jnp.int32, (rows, LANES), 0)
+    lane = lax.broadcasted_iota(jnp.int32, (rows, LANES), 1)
+    line = row % LINES
+    order = ones_where((line < 2) & (lane == row // LINES * 2 + line))
+    lines = jnp.dot(order, picked.astype(jnp.bfloat16), preferred_element_type=jnp.float32)
+    lines = jnp.where(line == 2, jnp.where(low, upper, middle), lines)
+    lines = jnp.where(line == 3, jnp.where(low, lower, center), lines)
+    out_ref[...] = lines.astype(jnp.bfloat16)
 
 
 def finish(all_ref, out_ref, lines_ref):
@@ -111,6 +156,10 @@
     return pltpu.with_memory_space_constraint(value, pltpu.VMEM)
 
 
+def exchanged(messages, groups):
+    return lax.all_to_all(messages, CORPUS, split_axis=0, concat_axis=0, axis_index_groups=groups, tiled=True)
+
+
 def body(queries, corpus, candidates):
     height, picks = candidates.shape
     size = lax.axis_size(CORPUS)
@@ -118,23 +167,31 @@
     both = lax.all_gather(corpus, "dim")
     sent = pl.pallas_call(
         functools.partial(pack, first),
-        out_shape=pltpu.VMEM((size * LINES, LANES), jnp.bfloat16),
+        out_shape=pltpu.VMEM((RING * MESSAGE, LANES), jnp.bfloat16),
         in_specs=[VMEM, VMEM, VMEM],
         out_specs=VMEM,
         name="pack",
     )(on_chip(queries), on_chip(both), on_chip(candidates))
-    ranks = [[rank ^ first for rank in range(size)]]
-    arrived = lax.all_to_all(
-        sent.reshape(size, LINES, LANES), CORPUS, split_axis=0, concat_axis=0, axis_index_groups=ranks, tiled=True
-    )
+    planes = size // RING
+    rings = [[plane * RING + (rank ^ (first % RING)) for rank in range(RING)] for plane in range(planes)]
+    ring = exchanged(sent.reshape(RING, MESSAGE, LANES), rings)
+    merged = pl.pallas_call(
+        merge,
+        out_shape=pltpu.VMEM((planes * LINES, LANES), jnp.bfloat16),
+        in_specs=[VMEM],
+        out_specs=VMEM,
+        name="merge",
+    )(on_chip(ring.reshape(RING * MESSAGE, LANES)))
+    groups = [[(rank ^ (first // RING)) * RING + near for rank in range(planes)] for near in range(RING)]
+    arrived = exchanged(merged.reshape(planes, LINES, LANES), groups)
     out = pl.pallas_call(
         finish,
         out_shape=jax.ShapeDtypeStruct((picks // size, height), jnp.float32),
         in_specs=[VMEM],
         out_specs=VMEM,
-        scratch_shapes=[pltpu.VMEM((size * LINES, LANES), jnp.float32)],
+        scratch_shapes=[pltpu.VMEM((planes * LINES, LANES), jnp.float32)],
         name="finish",
-    )(on_chip(arrived.reshape(size * LINES, LANES)))
+    )(on_chip(arrived.reshape(planes * LINES, LANES)))
     return out.T
 
 

time: 36.3 us -> 36 us (level)
  the two profiles are of different devices: /device:TPU:1 before, /device:TPU:2 now
where the time goes in v6:
time: 36 us; the launch traced here: 35.8 us
  blocking collectives  33.4 us (93%)
  Pallas kernels  2.31 us (6%)
    all_to_all x2, blocking collectives, exchanged(): lax.all_to_all(messages, CORPUS, split_axis=0, concat_axis=0, axis_index_...  30.7 us
    all_gather x1, blocking collectives, body(): both = lax.all_gather(corpus, 'dim')  2.7 us
    pallas_call x1, Pallas kernels, body(): pl.pallas_call(functools.partial(pack, first), out_shape=pltpu.VMEM((RING...  1.17 us
    pallas_call x1, Pallas kernels, body(): pl.pallas_call(finish, out_shape=jax.ShapeDtypeStruct((picks // size, hei...  0.84 us

profile of v6, /device:TPU:2, one launch (start us, length us, event | category | flops | bytes accessed | tf_op | source)
XLA Modules:
  0.0 35.8 jit_solution(5386381476293279954)
XLA Ops:
  0.0 0.0 copy-start
  0.0 0.0 copy-start.1
  0.0 2.7 %all-gather = bf16[1024,384]{1,0:T(8,128)(2,1)S(1)} all-gather(bf16[512,384]{1,0:T(8,128)(2,1)} %param.4), channel_id=2, replica_groups=mesh['corpus_0'=8,'corpus_1'=8,'corpus_2'=4,'dim'=2] {'dim'}, dimensions={0}, use_global_device_ids=true | all-gather | bytes 1179648 | tf_op jit(solution)/shard_map/all_gather | solution.py:167
  2.7 0.0 copy-done
  2.7 0.0 copy-done.1
  2.7 1.2 %pack.1 = bf16[576,128]{1,0:T(8,128)(2,1)S(1)} custom-call(bf16[64,768]{1,0:T(8,128)(2,1)S(1)} %copy-done.1, bf16[2,512,384]{2,1,0:T(8,128)(2,1)S(1)} %bitcast.6, s32[64,1024]{1,0:T(8,128)S(1)} %copy-done), custom_call_target="tpu_custom_call" | custom-call | tf_op jit(solution)/shard_map/pack/pallas_call | solution.py:168
  3.9 13.0 %all_to_all.10 = bf16[4,144,128]{2,1,0:T(8,128)(2,1)S(1)} all-to-all(bf16[4,144,128]{2,1,0:T(8,128)(2,1)S(1)} %bitcast.7), channel_id=1, replica_groups={{4,6,0,2},{12,14,8,10},{20,22,16,18},{28,30,24,26},{36,38,32,34},{44,46..., dimensions={0} | all-to-all | bytes 294912 | tf_op jit(solution)/shard_map/all_to_all | solution.py:160
  16.9 0.3 merge.1
  17.2 17.8 %all_to_all.11 = bf16[64,4,128]{2,1,0:T(4,128)(2,1)S(1)} all-to-all(bf16[64,4,128]{2,1,0:T(4,128)(2,1)S(1)} %bitcast.9), channel_id=1, replica_groups={{288,296,304,312,256,264,272,280,352,360,368,376,320,328,336,344,416,42..., dimensions={0} | all-to-all | bytes 131072 | tf_op jit(solution)/shard_map/all_to_all | solution.py:160
  34.9 0.8 %finish.1 = f32[4,64]{1,0:T(4,128)} custom-call(bf16[256,128]{1,0:T(8,128)(2,1)S(1)} %bitcast.10), custom_call_target="tpu_custom_call" | custom-call | tf_op jit(solution)/shard_map/finish/pallas_call | solution.py:187
Async XLA Ops:
  0.0 2.7 %copy-start = (s32[64,1024]{1,0:T(8,128)S(1)}, s32[64,1024]{1,0:T(8,128)}, u32[]{:S(2)}) copy-start(s32[64,1024]{1,0:T(8,128)} %candidates_ref.1) | copy-start | bytes 786436
  0.0 2.7 %copy-start.1 = (bf16[64,768]{1,0:T(8,128)(2,1)S(1)}, bf16[64,768]{1,0:T(8,128)(2,1)}, u32[]{:S(2)}) copy-start(bf16[64,768]{1,0:T(8,128)(2,1)} %queries_ref.1) | copy-start | bytes 294916

commit v7 on v6

--- a/solution.py
+++ b/solution.py
@@ -14,7 +14,8 @@
 LINES = 4
 RING = 4
 TILE = 16
-MESSAGE = LANES + TILE
+STATS = 8
+MESSAGE = LANES + STATS
 TINY = 1e-30
 FIRST = (4, 4, 2)
 
@@ -83,10 +84,10 @@
     for tile in range(candidates_ref.shape[1] // LANES):
         local = candidates_ref[:, tile * LANES : (tile + 1) * LANES] - offset
         block, lane = local >> 7, local & (LANES - 1)
-        value = jnp.zeros((height, LANES), jnp.float32)
+        value = jnp.zeros((height, LANES), jnp.bfloat16)
         for w in range(count // LANES):
-            value = jnp.where(block == w, lane_gather(moved[:, w * LANES : (w + 1) * LANES], lane), value)
-        value = value.astype(jnp.bfloat16)
+            got = lane_gather(moved[:, w * LANES : (w + 1) * LANES], lane).astype(jnp.bfloat16)
+            value = jnp.where(block == w, got, value)
         both = jnp.concatenate(
             [jnp.concatenate([value, nothing], axis=0), jnp.concatenate([nothing, value], axis=0)], axis=1
         )
@@ -94,8 +95,8 @@
         at = TILE * (tile ^ (first // RING // 8))
         for near in range(RING):
             out_ref[near * MESSAGE + at : near * MESSAGE + at + TILE, :] = lines[near * TILE : (near + 1) * TILE]
-    row = lax.broadcasted_iota(jnp.int32, (TILE, LANES), 0)
-    lane = lax.broadcasted_iota(jnp.int32, (TILE, LANES), 1)
+    row = lax.broadcasted_iota(jnp.int32, (STATS, LANES), 0)
+    lane = lax.broadcasted_iota(jnp.int32, (STATS, LANES), 1)
     last = matmul_nt(ones_where((row < 2) & (lane == row * HALF)), stats).astype(jnp.bfloat16)
     for near in range(RING):
         out_ref[near * MESSAGE + LANES : (near + 1) * MESSAGE, :] = last

time: 36 us -> 36 us (level)
  no operation moved by 1% of the time
where the time goes in v7:
time: 36 us; the launch traced here: 35.8 us
  blocking collectives  33.5 us (93%)
  Pallas kernels  2.32 us (6%)
    all_to_all x2, blocking collectives, exchanged(): lax.all_to_all(messages, CORPUS, split_axis=0, concat_axis=0, axis_index_...  30.8 us
    all_gather x1, blocking collectives, body(): both = lax.all_gather(corpus, 'dim')  2.7 us
    pallas_call x1, Pallas kernels, body(): pl.pallas_call(functools.partial(pack, first), out_shape=pltpu.VMEM((RING...  1.17 us
    pallas_call x1, Pallas kernels, body(): pl.pallas_call(finish, out_shape=jax.ShapeDtypeStruct((picks // size, hei...  0.84 us

profile of v7, /device:TPU:2, one launch (start us, length us, event | category | flops | bytes accessed | tf_op | source)
XLA Modules:
  0.0 35.8 jit_solution(6125619766920376036)
XLA Ops:
  0.0 0.0 copy-start
  0.0 0.0 copy-start.1
  0.0 2.7 %all-gather = bf16[1024,384]{1,0:T(8,128)(2,1)S(1)} all-gather(bf16[512,384]{1,0:T(8,128)(2,1)} %param.4), channel_id=2, replica_groups=mesh['corpus_0'=8,'corpus_1'=8,'corpus_2'=4,'dim'=2] {'dim'}, dimensions={0}, use_global_device_ids=true | all-gather | bytes 1179648 | tf_op jit(solution)/shard_map/all_gather | solution.py:168
  2.7 0.0 copy-done
  2.7 0.0 copy-done.1
  2.7 1.2 %pack.1 = bf16[544,128]{1,0:T(8,128)(2,1)S(1)} custom-call(bf16[64,768]{1,0:T(8,128)(2,1)S(1)} %copy-done.1, bf16[2,512,384]{2,1,0:T(8,128)(2,1)S(1)} %bitcast.6, s32[64,1024]{1,0:T(8,128)S(1)} %copy-done), custom_call_target="tpu_custom_call" | custom-call | tf_op jit(solution)/shard_map/pack/pallas_call | solution.py:169
  3.9 12.9 %all_to_all.10 = bf16[4,136,128]{2,1,0:T(8,128)(2,1)S(1)} all-to-all(bf16[4,136,128]{2,1,0:T(8,128)(2,1)S(1)} %bitcast.7), channel_id=1, replica_groups={{4,6,0,2},{12,14,8,10},{20,22,16,18},{28,30,24,26},{36,38,32,34},{44,46..., dimensions={0} | all-to-all | bytes 278528 | tf_op jit(solution)/shard_map/all_to_all | solution.py:161
  16.8 0.3 merge.1
  17.1 17.8 %all_to_all.11 = bf16[64,4,128]{2,1,0:T(4,128)(2,1)S(1)} all-to-all(bf16[64,4,128]{2,1,0:T(4,128)(2,1)S(1)} %bitcast.9), channel_id=1, replica_groups={{288,296,304,312,256,264,272,280,352,360,368,376,320,328,336,344,416,42..., dimensions={0} | all-to-all | bytes 131072 | tf_op jit(solution)/shard_map/all_to_all | solution.py:161
  35.0 0.8 %finish.1 = f32[4,64]{1,0:T(4,128)} custom-call(bf16[256,128]{1,0:T(8,128)(2,1)S(1)} %bitcast.10), custom_call_target="tpu_custom_call" | custom-call | tf_op jit(solution)/shard_map/finish/pallas_call | solution.py:188
Async XLA Ops:
  0.0 2.7 %copy-start = (s32[64,1024]{1,0:T(8,128)S(1)}, s32[64,1024]{1,0:T(8,128)}, u32[]{:S(2)}) copy-start(s32[64,1024]{1,0:T(8,128)} %candidates_ref.1) | copy-start | bytes 786436
  0.0 2.7 %copy-start.1 = (bf16[64,768]{1,0:T(8,128)(2,1)S(1)}, bf16[64,768]{1,0:T(8,128)(2,1)}, u32[]{:S(2)}) copy-start(bf16[64,768]{1,0:T(8,128)(2,1)} %queries_ref.1) | copy-start | bytes 294916

commit v8 on v7

--- a/solution.py
+++ b/solution.py
@@ -66,14 +66,21 @@
 
 
 def pack(first, queries_ref, corpus_ref, candidates_ref, out_ref):
-    width = corpus_ref.shape[2]
-    scores = matmul_nt(queries_ref[:, :width], corpus_ref[0]) + matmul_nt(queries_ref[:, width:], corpus_ref[1])
-    height, count = scores.shape
+    _, count, width = corpus_ref.shape
+    height = queries_ref.shape[0]
+    part = count // 2
+    scores = [
+        matmul_nt(queries_ref[:, :width], corpus_ref[0, k * part : (k + 1) * part])
+        + matmul_nt(queries_ref[:, width:], corpus_ref[1, k * part : (k + 1) * part])
+        for k in range(2)
+    ]
+    center = rounded(jnp.sum(scores[0], axis=1, keepdims=True) * (1.0 / part))
+    moved = [kept_off_zero(score - center) for score in scores]
+    tables = [moved[w * LANES // part][:, w * LANES % part : w * LANES % part + LANES] for w in range(count // LANES)]
     order = ring_order(first)
-    peak = jnp.max(scores, axis=1, keepdims=True)
-    lse = peak + jnp.log(jnp.sum(jnp.exp(scores - peak), axis=1, keepdims=True))
-    center = rounded(jnp.sum(scores, axis=1, keepdims=True) * (1.0 / count))
-    moved = kept_off_zero(scores - center)
+    peak = jnp.max(jnp.maximum(scores[0], scores[1]), axis=1, keepdims=True)
+    mass = jnp.sum(jnp.exp(scores[0] - peak) + jnp.exp(scores[1] - peak), axis=1, keepdims=True)
+    lse = peak + jnp.log(mass)
     upper = rounded(lse)
     middle = rounded(lse - upper)
     lower = lse - upper - middle
@@ -86,7 +93,7 @@
         block, lane = local >> 7, local & (LANES - 1)
         value = jnp.zeros((height, LANES), jnp.bfloat16)
         for w in range(count // LANES):
-            got = lane_gather(moved[:, w * LANES : (w + 1) * LANES], lane).astype(jnp.bfloat16)
+            got = lane_gather(tables[w], lane).astype(jnp.bfloat16)
             value = jnp.where(block == w, got, value)
         both = jnp.concatenate(
             [jnp.concatenate([value, nothing], axis=0), jnp.concatenate([nothing, value], axis=0)], axis=1

time: 36 us -> 35.9 us (level)
  no operation moved by 1% of the time
where the time goes in v8:
time: 35.9 us; the launch traced here: 35.8 us
  blocking collectives  33.5 us (93%)
  Pallas kernels  2.27 us (6%)
    all_to_all x2, blocking collectives, exchanged(): lax.all_to_all(messages, CORPUS, split_axis=0, concat_axis=0, axis_index_...  30.8 us
    all_gather x1, blocking collectives, body(): both = lax.all_gather(corpus, 'dim')  2.7 us
    pallas_call x1, Pallas kernels, body(): pl.pallas_call(functools.partial(pack, first), out_shape=pltpu.VMEM((RING...  1.12 us
    pallas_call x1, Pallas kernels, body(): pl.pallas_call(finish, out_shape=jax.ShapeDtypeStruct((picks // size, hei...  0.84 us

profile of v8, /device:TPU:2, one launch (start us, length us, event | category | flops | bytes accessed | tf_op | source)
XLA Modules:
  0.0 35.8 jit_solution(8086108476073465510)
XLA Ops:
  0.0 0.0 copy-start
  0.0 0.0 copy-start.1
  0.0 2.7 %all-gather = bf16[1024,384]{1,0:T(8,128)(2,1)S(1)} all-gather(bf16[512,384]{1,0:T(8,128)(2,1)} %param.4), channel_id=2, replica_groups=mesh['corpus_0'=8,'corpus_1'=8,'corpus_2'=4,'dim'=2] {'dim'}, dimensions={0}, use_global_device_ids=true | all-gather | bytes 1179648 | tf_op jit(solution)/shard_map/all_gather | solution.py:175
  2.7 0.0 copy-done
  2.7 0.0 copy-done.1
  2.7 1.1 %pack.1 = bf16[544,128]{1,0:T(8,128)(2,1)S(1)} custom-call(bf16[64,768]{1,0:T(8,128)(2,1)S(1)} %copy-done.1, bf16[2,512,384]{2,1,0:T(8,128)(2,1)S(1)} %bitcast.6, s32[64,1024]{1,0:T(8,128)S(1)} %copy-done), custom_call_target="tpu_custom_call" | custom-call | tf_op jit(solution)/shard_map/pack/pallas_call | solution.py:176
  3.8 12.9 %all_to_all.10 = bf16[4,136,128]{2,1,0:T(8,128)(2,1)S(1)} all-to-all(bf16[4,136,128]{2,1,0:T(8,128)(2,1)S(1)} %bitcast.7), channel_id=1, replica_groups={{4,6,0,2},{12,14,8,10},{20,22,16,18},{28,30,24,26},{36,38,32,34},{44,46..., dimensions={0} | all-to-all | bytes 278528 | tf_op jit(solution)/shard_map/all_to_all | solution.py:168
  16.8 0.3 merge.1
  17.1 17.8 %all_to_all.11 = bf16[64,4,128]{2,1,0:T(4,128)(2,1)S(1)} all-to-all(bf16[64,4,128]{2,1,0:T(4,128)(2,1)S(1)} %bitcast.9), channel_id=1, replica_groups={{288,296,304,312,256,264,272,280,352,360,368,376,320,328,336,344,416,42..., dimensions={0} | all-to-all | bytes 131072 | tf_op jit(solution)/shard_map/all_to_all | solution.py:168
  34.9 0.8 %finish.1 = f32[4,64]{1,0:T(4,128)} custom-call(bf16[256,128]{1,0:T(8,128)(2,1)S(1)} %bitcast.10), custom_call_target="tpu_custom_call" | custom-call | tf_op jit(solution)/shard_map/finish/pallas_call | solution.py:195
Async XLA Ops:
  0.0 2.7 %copy-start = (s32[64,1024]{1,0:T(8,128)S(1)}, s32[64,1024]{1,0:T(8,128)}, u32[]{:S(2)}) copy-start(s32[64,1024]{1,0:T(8,128)} %candidates_ref.1) | copy-start | bytes 786436
  0.0 2.7 %copy-start.1 = (bf16[64,768]{1,0:T(8,128)(2,1)S(1)}, bf16[64,768]{1,0:T(8,128)(2,1)}, u32[]{:S(2)}) copy-start(bf16[64,768]{1,0:T(8,128)(2,1)} %queries_ref.1) | copy-start | bytes 294916

commit v9 on v8

--- a/solution.py
+++ b/solution.py
@@ -89,12 +89,16 @@
     offset = lax.axis_index(CORPUS) * count
     nothing = jnp.zeros((height, LANES), jnp.bfloat16)
     for tile in range(candidates_ref.shape[1] // LANES):
-        local = candidates_ref[:, tile * LANES : (tile + 1) * LANES] - offset
-        block, lane = local >> 7, local & (LANES - 1)
-        value = jnp.zeros((height, LANES), jnp.bfloat16)
-        for w in range(count // LANES):
-            got = lane_gather(tables[w], lane).astype(jnp.bfloat16)
-            value = jnp.where(block == w, got, value)
+        values = []
+        for top in range(0, height, 16):
+            local = candidates_ref[top : top + 16, tile * LANES : (tile + 1) * LANES] - offset
+            block, lane = local >> 7, local & (LANES - 1)
+            value = jnp.zeros(local.shape, jnp.bfloat16)
+            for w in range(count // LANES):
+                got = lane_gather(tables[w][top : top + 16], lane).astype(jnp.bfloat16)
+                value = jnp.where(block == w, got, value)
+            values.append(value)
+        value = jnp.concatenate(values, axis=0)
         both = jnp.concatenate(
             [jnp.concatenate([value, nothing], axis=0), jnp.concatenate([nothing, value], axis=0)], axis=1
         )
@@ -112,19 +116,18 @@
 def merge(ring_ref, out_ref):
     low = lax.broadcasted_iota(jnp.int32, (1, LANES), 1) < HALF
     stats = [ring_ref[k * MESSAGE + LANES : (k + 1) * MESSAGE, :].astype(jnp.float32) for k in range(RING)]
-    locals_, centers = [], []
-    for stat in stats:
-        one, two = stat[0:1], stat[1:2]
-        turned = pltpu.roll(two, HALF, 1)
-        locals_.append(one + pltpu.roll(one, HALF, 1) + jnp.where(low, two, turned))
-        centers.append(jnp.where(low, turned, two))
-    peak = functools.reduce(jnp.maximum, locals_)
-    lse = peak + jnp.log(sum(jnp.exp(local - peak) for local in locals_))
-    center = rounded(sum(centers) * (1.0 / RING))
+    one = jnp.concatenate([stat[0:1] for stat in stats], axis=0)
+    two = jnp.concatenate([stat[1:2] for stat in stats], axis=0)
+    turned = pltpu.roll(two, HALF, 1)
+    local = one + pltpu.roll(one, HALF, 1) + jnp.where(low, two, turned)
+    peak = jnp.max(local, axis=0, keepdims=True)
+    lse = peak + jnp.log(jnp.sum(jnp.exp(local - peak), axis=0, keepdims=True))
+    centers = jnp.where(low, turned, two)
+    center = rounded(jnp.sum(centers, axis=0, keepdims=True) * (1.0 / RING))
     picked = jnp.zeros((LANES, LANES), jnp.float32)
     for k in range(RING):
         sent = ring_ref[k * MESSAGE : k * MESSAGE + LANES, :].astype(jnp.float32)
-        picked = jnp.where(sent != 0.0, kept_off_zero(sent + (centers[k] - center)), picked)
+        picked = jnp.where(sent != 0.0, kept_off_zero(sent + (centers[k : k + 1] - center)), picked)
     upper = rounded(lse)
     middle = rounded(lse - upper)
     lower = lse - upper - middle

time: 35.9 us -> 35.9 us (level)
  no operation moved by 1% of the time
where the time goes in v9:
time: 35.9 us; the launch traced here: 35.7 us
  blocking collectives  33.5 us (93%)
  Pallas kernels  2.27 us (6%)
    all_to_all x2, blocking collectives, exchanged(): lax.all_to_all(messages, CORPUS, split_axis=0, concat_axis=0, axis_index_...  30.8 us
    all_gather x1, blocking collectives, body(): both = lax.all_gather(corpus, 'dim')  2.7 us
    pallas_call x1, Pallas kernels, body(): pl.pallas_call(functools.partial(pack, first), out_shape=pltpu.VMEM((RING...  1.12 us
    pallas_call x1, Pallas kernels, body(): pl.pallas_call(finish, out_shape=jax.ShapeDtypeStruct((picks // size, hei...  0.84 us

profile of v9, /device:TPU:2, one launch (start us, length us, event | category | flops | bytes accessed | tf_op | source)
XLA Modules:
  0.0 35.7 jit_solution(2819492862107344115)
XLA Ops:
  0.0 0.0 copy-start
  0.0 0.0 copy-start.1
  0.0 2.7 %all-gather = bf16[1024,384]{1,0:T(8,128)(2,1)S(1)} all-gather(bf16[512,384]{1,0:T(8,128)(2,1)} %param.4), channel_id=2, replica_groups=mesh['corpus_0'=8,'corpus_1'=8,'corpus_2'=4,'dim'=2] {'dim'}, dimensions={0}, use_global_device_ids=true | all-gather | bytes 1179648 | tf_op jit(solution)/shard_map/all_gather | solution.py:178
  2.7 0.0 copy-done
  2.7 0.0 copy-done.1
  2.7 1.1 %pack.1 = bf16[544,128]{1,0:T(8,128)(2,1)S(1)} custom-call(bf16[64,768]{1,0:T(8,128)(2,1)S(1)} %copy-done.1, bf16[2,512,384]{2,1,0:T(8,128)(2,1)S(1)} %bitcast.6, s32[64,1024]{1,0:T(8,128)S(1)} %copy-done), custom_call_target="tpu_custom_call" | custom-call | tf_op jit(solution)/shard_map/pack/pallas_call | solution.py:179
  3.8 12.9 %all_to_all.10 = bf16[4,136,128]{2,1,0:T(8,128)(2,1)S(1)} all-to-all(bf16[4,136,128]{2,1,0:T(8,128)(2,1)S(1)} %bitcast.7), channel_id=1, replica_groups={{4,6,0,2},{12,14,8,10},{20,22,16,18},{28,30,24,26},{36,38,32,34},{44,46..., dimensions={0} | all-to-all | bytes 278528 | tf_op jit(solution)/shard_map/all_to_all | solution.py:171
  16.8 0.3 merge.1
  17.1 17.8 %all_to_all.11 = bf16[64,4,128]{2,1,0:T(4,128)(2,1)S(1)} all-to-all(bf16[64,4,128]{2,1,0:T(4,128)(2,1)S(1)} %bitcast.9), channel_id=1, replica_groups={{288,296,304,312,256,264,272,280,352,360,368,376,320,328,336,344,416,42..., dimensions={0} | all-to-all | bytes 131072 | tf_op jit(solution)/shard_map/all_to_all | solution.py:171
  34.9 0.8 %finish.1 = f32[4,64]{1,0:T(4,128)} custom-call(bf16[256,128]{1,0:T(8,128)(2,1)S(1)} %bitcast.10), custom_call_target="tpu_custom_call" | custom-call | tf_op jit(solution)/shard_map/finish/pallas_call | solution.py:198
Async XLA Ops:
  0.0 2.7 %copy-start = (s32[64,1024]{1,0:T(8,128)S(1)}, s32[64,1024]{1,0:T(8,128)}, u32[]{:S(2)}) copy-start(s32[64,1024]{1,0:T(8,128)} %candidates_ref.1) | copy-start | bytes 786436
  0.0 2.7 %copy-start.1 = (bf16[64,768]{1,0:T(8,128)(2,1)S(1)}, bf16[64,768]{1,0:T(8,128)(2,1)}, u32[]{:S(2)}) copy-start(bf16[64,768]{1,0:T(8,128)(2,1)} %queries_ref.1) | copy-start | bytes 294916

commit v10 on v9

--- a/solution.py
+++ b/solution.py
@@ -17,7 +17,7 @@
 STATS = 8
 MESSAGE = LANES + STATS
 TINY = 1e-30
-FIRST = (4, 4, 2)
+FIRST = (4, 5, 2)
 
 
 def first_rank(shape):

time: 35.9 us -> 35.9 us (level)
  no operation moved by 1% of the time
where the time goes in v10:
time: 35.9 us; the launch traced here: 35.8 us
  blocking collectives  33.5 us (93%)
  Pallas kernels  2.27 us (6%)
    all_to_all x2, blocking collectives, exchanged(): lax.all_to_all(messages, CORPUS, split_axis=0, concat_axis=0, axis_index_...  30.8 us
    all_gather x1, blocking collectives, body(): both = lax.all_gather(corpus, 'dim')  2.7 us
    pallas_call x1, Pallas kernels, body(): pl.pallas_call(functools.partial(pack, first), out_shape=pltpu.VMEM((RING...  1.12 us
    pallas_call x1, Pallas kernels, body(): pl.pallas_call(finish, out_shape=jax.ShapeDtypeStruct((picks // size, hei...  0.84 us

profile of v10, /device:TPU:2, one launch (start us, length us, event | category | flops | bytes accessed | tf_op | source)
XLA Modules:
  0.0 35.8 jit_solution(911861175161060110)
XLA Ops:
  0.0 0.0 copy-start
  0.0 0.0 copy-start.1
  0.0 2.7 %all-gather = bf16[1024,384]{1,0:T(8,128)(2,1)S(1)} all-gather(bf16[512,384]{1,0:T(8,128)(2,1)} %param.4), channel_id=2, replica_groups=mesh['corpus_0'=8,'corpus_1'=8,'corpus_2'=4,'dim'=2] {'dim'}, dimensions={0}, use_global_device_ids=true | all-gather | bytes 1179648 | tf_op jit(solution)/shard_map/all_gather | solution.py:178
  2.7 0.0 copy-done
  2.7 0.0 copy-done.1
  2.7 1.1 %pack.1 = bf16[544,128]{1,0:T(8,128)(2,1)S(1)} custom-call(bf16[64,768]{1,0:T(8,128)(2,1)S(1)} %copy-done.1, bf16[2,512,384]{2,1,0:T(8,128)(2,1)S(1)} %bitcast.6, s32[64,1024]{1,0:T(8,128)S(1)} %copy-done), custom_call_target="tpu_custom_call" | custom-call | tf_op jit(solution)/shard_map/pack/pallas_call | solution.py:179
  3.8 12.9 %all_to_all.10 = bf16[4,136,128]{2,1,0:T(8,128)(2,1)S(1)} all-to-all(bf16[4,136,128]{2,1,0:T(8,128)(2,1)S(1)} %bitcast.7), channel_id=1, replica_groups={{4,6,0,2},{12,14,8,10},{20,22,16,18},{28,30,24,26},{36,38,32,34},{44,46..., dimensions={0} | all-to-all | bytes 278528 | tf_op jit(solution)/shard_map/all_to_all | solution.py:171
  16.8 0.3 merge.1
  17.1 17.8 %all_to_all.11 = bf16[64,4,128]{2,1,0:T(4,128)(2,1)S(1)} all-to-all(bf16[64,4,128]{2,1,0:T(4,128)(2,1)S(1)} %bitcast.9), channel_id=1, replica_groups={{296,288,312,304,264,256,280,272,360,352,376,368,328,320,344,336,424,41..., dimensions={0} | all-to-all | bytes 131072 | tf_op jit(solution)/shard_map/all_to_all | solution.py:171
  34.9 0.8 %finish.1 = f32[4,64]{1,0:T(4,128)} custom-call(bf16[256,128]{1,0:T(8,128)(2,1)S(1)} %bitcast.10), custom_call_target="tpu_custom_call" | custom-call | tf_op jit(solution)/shard_map/finish/pallas_call | solution.py:198
Async XLA Ops:
  0.0 2.7 %copy-start = (s32[64,1024]{1,0:T(8,128)S(1)}, s32[64,1024]{1,0:T(8,128)}, u32[]{:S(2)}) copy-start(s32[64,1024]{1,0:T(8,128)} %candidates_ref.1) | copy-start | bytes 786436
  0.0 2.7 %copy-start.1 = (bf16[64,768]{1,0:T(8,128)(2,1)S(1)}, bf16[64,768]{1,0:T(8,128)(2,1)}, u32[]{:S(2)}) copy-start(bf16[64,768]{1,0:T(8,128)(2,1)} %queries_ref.1) | copy-start | bytes 294916

commit v11 on v10

--- a/solution.py
+++ b/solution.py
@@ -70,8 +70,8 @@
     height = queries_ref.shape[0]
     part = count // 2
     scores = [
-        matmul_nt(queries_ref[:, :width], corpus_ref[0, k * part : (k + 1) * part])
-        + matmul_nt(queries_ref[:, width:], corpus_ref[1, k * part : (k + 1) * part])
+        matmul_nt(queries_ref[:, :width], corpus_ref[1, k * part : (k + 1) * part])
+        + matmul_nt(queries_ref[:, width:], corpus_ref[0, k * part : (k + 1) * part])
         for k in range(2)
     ]
     center = rounded(jnp.sum(scores[0], axis=1, keepdims=True) * (1.0 / part))
@@ -175,7 +175,7 @@
     height, picks = candidates.shape
     size = lax.axis_size(CORPUS)
     first = first_rank([lax.axis_size(axis) for axis in CORPUS])
-    both = lax.all_gather(corpus, "dim")
+    both = lax.all_gather(corpus, "dim", axis_index_groups=[[1, 0]])
     sent = pl.pallas_call(
         functools.partial(pack, first),
         out_shape=pltpu.VMEM((RING * MESSAGE, LANES), jnp.bfloat16),

time: 35.9 us -> 35.9 us (level)
  no operation moved by 1% of the time
where the time goes in v11:
time: 35.9 us; the launch traced here: 35.8 us
  blocking collectives  33.5 us (93%)
  Pallas kernels  2.27 us (6%)
    all_to_all x2, blocking collectives, exchanged(): lax.all_to_all(messages, CORPUS, split_axis=0, concat_axis=0, axis_index_...  30.8 us
    all_gather x1, blocking collectives, body(): both = lax.all_gather(corpus, 'dim', axis_index_groups=[[1, 0]])  2.7 us
    pallas_call x1, Pallas kernels, body(): pl.pallas_call(functools.partial(pack, first), out_shape=pltpu.VMEM((RING...  1.12 us
    pallas_call x1, Pallas kernels, body(): pl.pallas_call(finish, out_shape=jax.ShapeDtypeStruct((picks // size, hei...  0.84 us

profile of v11, /device:TPU:2, one launch (start us, length us, event | category | flops | bytes accessed | tf_op | source)
XLA Modules:
  0.0 35.8 jit_solution(4395382552895248072)
XLA Ops:
  0.0 0.0 copy-start
  0.0 0.0 copy-start.1
  0.0 2.7 %all-gather = bf16[1024,384]{1,0:T(8,128)(2,1)S(1)} all-gather(bf16[512,384]{1,0:T(8,128)(2,1)} %param.4), channel_id=2, replica_groups={{1,0},{3,2},{5,4},{7,6},{9,8},{11,10},{13,12},{15,14},{17,16},{19,18},{..., dimensions={0}, use_global_device_ids=true | all-gather | bytes 1179648 | tf_op jit(solution)/shard_map/all_gather | solution.py:178
  2.7 0.0 copy-done
  2.7 0.0 copy-done.1
  2.7 1.1 %pack.1 = bf16[544,128]{1,0:T(8,128)(2,1)S(1)} custom-call(bf16[64,768]{1,0:T(8,128)(2,1)S(1)} %copy-done.1, bf16[2,512,384]{2,1,0:T(8,128)(2,1)S(1)} %bitcast.6, s32[64,1024]{1,0:T(8,128)S(1)} %copy-done), custom_call_target="tpu_custom_call" | custom-call | tf_op jit(solution)/shard_map/pack/pallas_call | solution.py:179
  3.8 12.9 %all_to_all.10 = bf16[4,136,128]{2,1,0:T(8,128)(2,1)S(1)} all-to-all(bf16[4,136,128]{2,1,0:T(8,128)(2,1)S(1)} %bitcast.7), channel_id=1, replica_groups={{4,6,0,2},{12,14,8,10},{20,22,16,18},{28,30,24,26},{36,38,32,34},{44,46..., dimensions={0} | all-to-all | bytes 278528 | tf_op jit(solution)/shard_map/all_to_all | solution.py:171
  16.8 0.3 merge.1
  17.1 17.8 %all_to_all.11 = bf16[64,4,128]{2,1,0:T(4,128)(2,1)S(1)} all-to-all(bf16[64,4,128]{2,1,0:T(4,128)(2,1)S(1)} %bitcast.9), channel_id=1, replica_groups={{296,288,312,304,264,256,280,272,360,352,376,368,328,320,344,336,424,41..., dimensions={0} | all-to-all | bytes 131072 | tf_op jit(solution)/shard_map/all_to_all | solution.py:171
  34.9 0.8 %finish.1 = f32[4,64]{1,0:T(4,128)} custom-call(bf16[256,128]{1,0:T(8,128)(2,1)S(1)} %bitcast.10), custom_call_target="tpu_custom_call" | custom-call | tf_op jit(solution)/shard_map/finish/pallas_call | solution.py:198
Async XLA Ops:
  0.0 2.7 %copy-start = (s32[64,1024]{1,0:T(8,128)S(1)}, s32[64,1024]{1,0:T(8,128)}, u32[]{:S(2)}) copy-start(s32[64,1024]{1,0:T(8,128)} %candidates_ref.1) | copy-start | bytes 786436
  0.0 2.7 %copy-start.1 = (bf16[64,768]{1,0:T(8,128)(2,1)S(1)}, bf16[64,768]{1,0:T(8,128)(2,1)}, u32[]{:S(2)}) copy-start(bf16[64,768]{1,0:T(8,128)(2,1)} %queries_ref.1) | copy-start | bytes 294916
